TPU v7x, 32 devices: a whole 2x2x4 slice. The times are simulated.
32 devices in a mesh: seq: 16 (over z, x, core), head: 2 (over y).
Axes of the slice: x: 2, y: 2, z: 4, core: 2. Of those that a mesh axis runs over, the one named last changes fastest.
Arguments:
- query: bfloat16 [1, 4096, 2048], P(None, 'seq', 'head'), may hold values from -210 to 210
- keys: bfloat16 [1, 4096, 512], P(None, 'seq', 'head'), may hold values from -7 to 7
- values: bfloat16 [1, 4096, 512], P(None, 'seq', 'head'), may hold values from -6 to 6
- grad_out: bfloat16 [1, 4096, 2048], P(None, 'seq', 'head'), may hold values from -6 to 6
- global_offset: int32 [1, 64], replicated, may hold values from 0 to 255, as said below
- owner: int32 [16], replicated, may hold values from 0 to 15, each once
- block_lists: int32 [1, 32, 3], P(None, 'seq'), may hold values from 0 to 31, as said below
Outputs:
- grad_query: bfloat16 [1, 4096, 2048], P(None, 'seq', 'head')
- grad_keys: bfloat16 [1, 4096, 512], P(None, 'seq', 'head')
- grad_values: bfloat16 [1, 4096, 512], P(None, 'seq', 'head')
Inputs may be any that keep to these rules, and one draw needn't show every extreme that they name: `block_lists`: row b of each layer lists b first, then 3 - 1 other distinct blocks within 2 blocks of b. `global_offset`: distinct within a layer. `owner`: each sequence shard appears once.
All inputs are finite; a program needn't handle non-finite values.
Results may differ from a plain program's by a relative error of at most 0.02.
Values may be sent and summed in bfloat16 or wider, within the bound.
A program may use at most 64 MiB of HBM per device.

v0:
```python
import functools

import jax
import jax.numpy as jnp
from jax import lax
from jax.experimental import pallas as pl
from jax.experimental.pallas import tpu as pltpu
from jax.sharding import PartitionSpec as P

HQ = 16
HK = 4
DH = 128
BLOCK = 128
REACH = 2
PIECE = 32
LOG2E = 1.4426950408889634
F32 = jnp.float32
BF16 = jnp.bfloat16


def nt(a, b):
    return lax.dot_general(a, b, (((1,), (1,)), ((), ())), preferred_element_type=F32)


def nn(a, b):
    return lax.dot_general(a, b, (((1,), (0,)), ((), ())), preferred_element_type=F32)


def kernel(
    n, heads, group, nb, listed, gtok,
    owner_ref, lists_ref, goff_ref, q_hbm, k_hbm, v_hbm, g_hbm,
    dq_ref, dk_ref, dv_ref,
    qv, gv, gsend, hub_in, hub_out, gall, gpart, hub2_in, hub2_out, gall2,
    keep_ex, keep_dp, keep_ds, wslot, own, sback, rback, load_sem, big_sem, ks_sem, kr_sem, gs_sem, gr_sem, hs_sem, hr_sem,
    *kvw,
):
    me = lax.axis_index("seq")
    rpp = gtok // PIECE
    pieces = 2 * heads * rpp
    rows = nb * BLOCK
    src_refs = (k_hbm, v_hbm)

    loads = []
    for t in range(2):
        for c in range(heads):
            for i in range(nb):
                cp = pltpu.make_async_copy(
                    src_refs[t].at[0, pl.ds(i * BLOCK, BLOCK), pl.ds(c * DH, DH)],
                    kvw[t * heads + c].at[REACH + i],
                    load_sem.at[(t * heads + c) * nb + i],
                )
                cp.start()
                loads.append(cp)
    cq = pltpu.make_async_copy(q_hbm.at[0], qv, big_sem.at[0])
    cg = pltpu.make_async_copy(g_hbm.at[0], gv, big_sem.at[1])
    cq.start()
    cg.start()

    barrier = pltpu.get_barrier_semaphore()

    first = (n - pieces) // 2
    hub = me - first

    def hubbed(i):
        return (i >= first) & (i < first + pieces)

    @pl.loop(1, n)
    def _(i):
        other = lax.rem(me + i, n)

        @pl.when(hubbed(me) | hubbed(other) | (other == me + 1) | (other == me - 1))
        def _():
            pl.semaphore_signal(
                barrier, inc=1, device_id={"seq": other}, device_id_type=pl.DeviceIdType.MESH
            )

    for cp in loads:
        cp.wait()

    hot = lax.broadcasted_iota(jnp.int32, (rows, gtok), 0) == goff_ref[...]
    hot = jnp.where(hot, 1.0, 0.0).astype(BF16)
    for t in range(2):
        for c in range(heads):
            mine = kvw[t * heads + c][REACH : REACH + nb].reshape(rows, DH)
            got = lax.dot_general(hot, mine, (((0,), (0,)), ((), ())), preferred_element_type=F32)
            base = (t * heads + c) * rpp
            gsend[base : base + rpp] = got.astype(BF16).reshape(rpp, PIECE, DH)
    zeros_kv = jnp.zeros((REACH, BLOCK, DH), BF16)

    @pl.when(me == 0)
    def _():
        for ref in kvw:
            ref[0:REACH] = zeros_kv
        rback[0] = jnp.zeros(rback.shape[1:], BF16)

    @pl.when(me == n - 1)
    def _():
        for ref in kvw:
            ref[REACH + nb : REACH + nb + REACH] = zeros_kv
        rback[1] = jnp.zeros(rback.shape[1:], BF16)

    zero_tile = jnp.zeros((nb, 2, BLOCK, DH), F32)
    wslot[:, listed] = zero_tile

    below = jnp.where((me > 0) & ~hubbed(me - 1), 1, 0)
    above = jnp.where((me < n - 1) & ~hubbed(me + 1), 1, 0)
    pl.semaphore_wait(barrier, jnp.where(hubbed(me), n - 1, pieces + below + above))

    def remote(src, dst, s_sem, r_sem, target):
        return pltpu.make_async_remote_copy(
            src_ref=src, dst_ref=dst, send_sem=s_sem, recv_sem=r_sem,
            device_id={"seq": target}, device_id_type=pl.DeviceIdType.MESH,
        )

    def hub_send(src, dst, s_sem, r_sem, j):
        @pl.when(j != hub)
        def _():
            remote(src.at[j], dst.at[me], s_sem, r_sem, first + j).start()

    def drain(ref, count, sem):
        part = ref.at[pl.ds(0, count)]
        pltpu.make_async_copy(part, part, sem).wait()

    @pl.loop(0, pieces)
    def _(i):
        hub_send(gsend, hub_in, hs_sem.at[0], hr_sem.at[0], lax.rem(me + i, pieces))

    def halo(direction, c, t):
        idx = (direction * heads + c) * 2 + t
        ref = kvw[t * heads + c]
        if direction == 0:
            src, dst, target = ref.at[pl.ds(nb, REACH)], ref.at[pl.ds(0, REACH)], me + 1
        else:
            src, dst, target = ref.at[pl.ds(REACH, REACH)], ref.at[pl.ds(REACH + nb, REACH)], me - 1
        return remote(src, dst, ks_sem.at[idx], kr_sem.at[idx], target)

    def back(direction, c):
        idx = direction * heads + c
        target = me + 1 if direction == 0 else me - 1
        return remote(
            sback.at[direction, c], rback.at[direction, c], gs_sem.at[idx], gr_sem.at[idx], target
        )

    def each(direction, receiving, what):
        up = (direction == 0) != receiving
        cond = me < n - 1 if up else me > 0
        pl.when(cond)(what)

    for c in range(heads):
        for t in range(2):
            for d in range(2):
                each(d, False, lambda d=d, c=c, t=t: halo(d, c, t).start())

    @pl.when(hubbed(me))
    def _():
        hub_in[me] = gsend[hub]
        drain(hub_in, n - 1, hr_sem.at[0])
        pick = hub_in[owner_ref[0]]
        hub_out[...] = pick
        gall[hub] = pick

        @pl.loop(1, n)
        def _(i):
            remote(hub_out, gall.at[hub], hs_sem.at[1], hr_sem.at[1], lax.rem(me + i, n)).start()

    cq.wait()
    cg.wait()
    scale = DH ** (-0.5)
    fold = scale * LOG2E
    local_idx = [
        [
            jnp.clip(lists_ref[0, b, l] - me * nb + REACH, 0, nb + 2 * REACH - 1)
            for l in range(listed)
        ]
        for b in range(nb)
    ]

    def listed_rows(t, c, b):
        return jnp.concatenate([kvw[t * heads + c][local_idx[b][l]] for l in range(listed)], axis=0)

    def global_rows(ref, t, c):
        base = (t * heads + c) * rpp
        return ref[base : base + rpp].reshape(gtok, DH)

    def columns(c):
        return [slice((c * group + i) * DH, (c * group + i + 1) * DH) for i in range(group)]

    def stacked(ref, c, b):
        rsl = slice(b * BLOCK, (b + 1) * BLOCK)
        return jnp.concatenate([ref[rsl, s] for s in columns(c)], axis=0)

    stats = {}
    for c in range(heads):
        for t in range(2):
            for d in range(2):
                each(d, True, lambda d=d, c=c, t=t: halo(d, c, t).wait_recv())
        for b in range(nb):
            st = nt(listed_rows(0, c, b), stacked(qv, c, b))
            dp = nt(listed_rows(1, c, b), stacked(gv, c, b))
            top = jnp.max(st, axis=0, keepdims=True)
            ex = jnp.exp2((st - top) * fold)
            keep_ex[c, b] = ex
            keep_dp[c, b] = dp
            stats[c, b] = (
                top,
                jnp.sum(ex, axis=0, keepdims=True),
                jnp.sum(ex * dp, axis=0, keepdims=True),
            )

    @pl.when(hubbed(me))
    def _():
        drain(gall, pieces - 1, hr_sem.at[1])

    @pl.when(~hubbed(me))
    def _():
        drain(gall, pieces, hr_sem.at[1])

    for c in range(heads):
        kg, vg = global_rows(gall, 0, c), global_rows(gall, 1, c)
        glob = [None, None]
        for b in range(nb):
            qs, gs = stacked(qv, c, b), stacked(gv, c, b)
            st = nt(kg, qs)
            dp = nt(vg, gs)
            top_w, sum_w, dot_w = stats[c, b]
            top = jnp.maximum(top_w, jnp.max(st, axis=0, keepdims=True))
            ex = jnp.exp2((st - top) * fold)
            shrink = jnp.exp2((top_w - top) * fold)
            inv = 1.0 / (sum_w * shrink + jnp.sum(ex, axis=0, keepdims=True))
            dot = (dot_w * shrink + jnp.sum(ex * dp, axis=0, keepdims=True)) * inv
            pr = ex * inv
            ds = (pr * (dp - dot)).astype(BF16)
            keep_ds[c, b] = ds
            stats[c, b] = (shrink * inv, dot)
            for t, part in enumerate((nn(ds, qs) * scale, nn(pr.astype(BF16), gs))):
                glob[t] = part if glob[t] is None else glob[t] + part
        for t in range(2):
            base = (t * heads + c) * rpp
            gpart[base : base + rpp] = glob[t].astype(BF16).reshape(rpp, PIECE, DH)

    @pl.loop(0, pieces)
    def _(i):
        hub_send(gpart, hub2_in, hs_sem.at[2], hr_sem.at[2], lax.rem(me + i, pieces))

    for c in range(heads):
        for b in range(nb):
            qs, gs = stacked(qv, c, b), stacked(gv, c, b)
            ratio, dot = stats[c, b]
            pr = keep_ex[c, b] * ratio
            ds = (pr * (keep_dp[c, b] - dot)).astype(BF16)
            dv = nn(pr.astype(BF16), gs)
            dk = nn(ds, qs) * scale
            for t, val in enumerate((dk, dv)):
                for l in range(listed):
                    wslot[b, l, t] = val[l * BLOCK : (l + 1) * BLOCK]
            ks = jnp.concatenate([listed_rows(0, c, b), global_rows(gall, 0, c)], axis=0)
            dqt = nn(ks.T, jnp.concatenate([ds, keep_ds[c, b]], axis=0)) * scale
            dq = dqt.T.astype(BF16)
            for i, s in enumerate(columns(c)):
                dq_ref[0, b * BLOCK : (b + 1) * BLOCK, s] = dq[i * BLOCK : (i + 1) * BLOCK]
        for dst in range(nb + 2 * REACH):
            total = None
            for b in range(nb):
                if not b <= dst <= b + 2 * REACH:
                    continue
                slot = jnp.int32(listed)
                for l in range(listed):
                    slot = jnp.where(local_idx[b][l] == dst, l, slot)
                term = wslot[b, slot]
                total = term if total is None else total + term
            if dst < REACH:
                sback[1, c, dst] = total.astype(BF16)
            elif dst < REACH + nb:
                own[c, dst - REACH] = total
            else:
                sback[0, c, dst - REACH - nb] = total.astype(BF16)
        for d in range(2):
            each(d, False, lambda d=d, c=c: back(d, c).start())

    @pl.when(hubbed(me))
    def _():
        hub2_in[me] = gpart[hub]
        drain(hub2_in, n - 1, hr_sem.at[2])
        total = jnp.sum(hub2_in[...].astype(F32), axis=0).astype(BF16)
        hub2_out[...] = total
        gall2[hub] = total

        @pl.loop(1, n)
        def _(i):
            remote(hub2_out, gall2.at[hub], hs_sem.at[3], hr_sem.at[3], lax.rem(me + i, n)).start()

        drain(gall2, pieces - 1, hr_sem.at[3])

    @pl.when(~hubbed(me))
    def _():
        drain(gall2, pieces, hr_sem.at[3])

    flag = jnp.where(owner_ref[0] == me, 1.0, 0.0)
    for c in range(heads):
        for d in range(2):
            each(d, True, lambda d=d, c=c: back(d, c).wait_recv())
        for t, out in enumerate((dk_ref, dv_ref)):
            extra = nn(hot, global_rows(gall2, t, c)) * flag
            for i in range(nb):
                rsl = slice(i * BLOCK, (i + 1) * BLOCK)
                total = own[c, i, t] + extra[rsl]
                total = total + rback[0, c, i, t].astype(F32) + rback[1, c, i, t].astype(F32)
                out[0, rsl, c * DH : (c + 1) * DH] = total.astype(BF16)

    for c in range(heads):
        for d in range(2):
            for t in range(2):
                each(d, False, lambda d=d, c=c, t=t: halo(d, c, t).wait_send())
            each(d, False, lambda d=d, c=c: back(d, c).wait_send())

    @pl.when(hubbed(me))
    def _():
        drain(gsend, pieces - 1, hs_sem.at[0])
        drain(gpart, pieces - 1, hs_sem.at[2])
        drain(hub_in, n - 1, hs_sem.at[1])
        drain(hub2_in, n - 1, hs_sem.at[3])

    @pl.when(~hubbed(me))
    def _():
        drain(gsend, pieces, hs_sem.at[0])
        drain(gpart, pieces, hs_sem.at[2])


def write_out(*refs):
    copies = [
        pltpu.make_async_copy(refs[i], refs[3 + i], refs[6].at[i]) for i in range(3)
    ]
    for cp in copies:
        cp.start()
    for cp in copies:
        cp.wait()


def solution(mesh):
    n = mesh.shape["seq"]

    def local(query, keys, values, grad_out, global_offset, owner, block_lists):
        rows, qw = query.shape[1:]
        kw = keys.shape[2]
        heads = kw // DH
        group = HQ // HK
        nb = rows // BLOCK
        listed = block_lists.shape[2]
        gtok = global_offset.shape[1]
        pieces = 2 * heads * gtok // PIECE
        wide = nb + 2 * REACH
        assert nb == REACH and n >= pieces
        vm = pl.BlockSpec(memory_space=pltpu.VMEM)
        sm = pl.BlockSpec(memory_space=pltpu.SMEM)
        hb = pl.BlockSpec(memory_space=pl.ANY)
        held = pl.pallas_call(
            functools.partial(kernel, n, heads, group, nb, listed, gtok),
            out_shape=tuple(pltpu.VMEM(a.shape, BF16) for a in (query, keys, values)),
            in_specs=[sm, sm, vm, hb, hb, hb, hb],
            out_specs=(vm, vm, vm),
            scratch_shapes=[
                pltpu.VMEM((rows, qw), BF16),
                pltpu.VMEM((rows, qw), BF16),
                pltpu.VMEM((pieces, PIECE, DH), BF16),
                pltpu.VMEM((n, PIECE, DH), BF16),
                pltpu.VMEM((PIECE, DH), BF16),
                pltpu.VMEM((pieces, PIECE, DH), BF16),
                pltpu.VMEM((pieces, PIECE, DH), BF16),
                pltpu.VMEM((n, PIECE, DH), BF16),
                pltpu.VMEM((PIECE, DH), BF16),
                pltpu.VMEM((pieces, PIECE, DH), BF16),
                pltpu.VMEM((heads, nb, listed * BLOCK, group * BLOCK), F32),
                pltpu.VMEM((heads, nb, listed * BLOCK, group * BLOCK), F32),
                pltpu.VMEM((heads, nb, gtok, group * BLOCK), BF16),
                pltpu.VMEM((nb, listed + 1, 2, BLOCK, DH), F32),
                pltpu.VMEM((heads, nb, 2, BLOCK, DH), F32),
                pltpu.VMEM((2, heads, REACH, 2, BLOCK, DH), BF16),
                pltpu.VMEM((2, heads, REACH, 2, BLOCK, DH), BF16),
                pltpu.SemaphoreType.DMA((2 * heads * nb,)),
                pltpu.SemaphoreType.DMA((2,)),
                pltpu.SemaphoreType.DMA((4 * heads,)),
                pltpu.SemaphoreType.DMA((4 * heads,)),
                pltpu.SemaphoreType.DMA((2 * heads,)),
                pltpu.SemaphoreType.DMA((2 * heads,)),
                pltpu.SemaphoreType.DMA((4,)),
                pltpu.SemaphoreType.DMA((4,)),
            ]
            + [pltpu.VMEM((wide, BLOCK, DH), BF16)] * (2 * heads),
            compiler_params=pltpu.CompilerParams(collective_id=0, has_side_effects=True),
        )(owner, block_lists, global_offset, query, keys, values, grad_out)
        return pl.pallas_call(
            write_out,
            out_shape=tuple(jax.ShapeDtypeStruct(a.shape, BF16) for a in (query, keys, values)),
            in_specs=[hb] * 3,
            out_specs=[hb] * 3,
            scratch_shapes=[pltpu.SemaphoreType.DMA((3,))],
        )(*[pltpu.with_memory_space_constraint(a, pltpu.VMEM) for a in held])

    return jax.shard_map(
        local,
        mesh=mesh,
        in_specs=(
            P(None, "seq", "head"),
            P(None, "seq", "head"),
            P(None, "seq", "head"),
            P(None, "seq", "head"),
            P(),
            P(),
            P(None, "seq", None),
        ),
        out_specs=(P(None, "seq", "head"), P(None, "seq", "head"), P(None, "seq", "head")),
        check_vma=False,
    )
```

profile of v0, /device:TPU:0, one launch (start us, length us, event | category | flops | bytes accessed | tf_op | source)
XLA Modules:
  0.0 28.1 jit_solution(13753693860043119496)
XLA Ops:
  0.6 26.5 %shard_map.94 = (bf16[1,256,1024]{2,1,0:T(8,128)(2,1)S(1)}, bf16[1,256,256]{2,1,0:T(8,128)(2,1)S(1)}, bf16[1,256,256]{2,1,0:T(8,128)(2,1)S(1)}) custom-call(s32[16]{0:T(128)} %owner_ref.1, s32[1,2,3]{2,1,0:T(2,128)} %lists_ref.1, s32[1,64]{1,0:T(1,128)} %goff_ref.1, bf16[1,256,1024]{2,1,0:T(8,128)(2,1)} %q_hbm.1, bf16[1,256,256]{2,1,0:T(8,128)(2,1)} %k_hbm.1, ...), custom_call_target="tpu_custom_call" | custom-call | tf_op jit(solution)/shard_map/pallas_call | solution.py:356
  27.2 0.9 %shard_map.95 = (bf16[1,256,1024]{2,1,0:T(8,128)(2,1)}, bf16[1,256,256]{2,1,0:T(8,128)(2,1)}, bf16[1,256,256]{2,1,0:T(8,128)(2,1)}) custom-call(bf16[1,256,1024]{2,1,0:T(8,128)(2,1)S(1)} %get-tuple-element.6.refs_0_, bf16[1,256,256]{2,1,0:T(8,128)(2,1)S(1)} %get-tuple-element.7.refs_1_, bf16[1,256,256]{2,1,0:T(8,128)(2,1)S(1)} %get-tuple-element.8.refs_2_), custom_call_target="tpu_custom_call" | custom-call | tf_op jit(solution)/shard_map/pallas_call | solution.py:391
where the time goes:
time: 28.2 us; the launch traced here: 28.1 us
  Pallas kernels  27.4 us (97%)
  between operations  0.64 us (2%)
    pallas_call x1, Pallas kernels, local(): pl.pallas_call(functools.partial(kernel, n, heads, group, nb, listed, gto...  26.5 us
    pallas_call x1, Pallas kernels, local(): pl.pallas_call(write_out, out_shape=tuple((jax.ShapeDtypeStruct(a.shape,...  0.9 us

commit v1 on v0

--- a/solution.py
+++ b/solution.py
@@ -12,7 +12,6 @@
 DH = 128
 BLOCK = 128
 REACH = 2
-PIECE = 32
 LOG2E = 1.4426950408889634
 F32 = jnp.float32
 BF16 = jnp.bfloat16
@@ -28,18 +27,55 @@
 
 def kernel(
     n, heads, group, nb, listed, gtok,
-    owner_ref, lists_ref, goff_ref, q_hbm, k_hbm, v_hbm, g_hbm,
+    owner_hbm, lists_hbm, goff_hbm, q_hbm, k_hbm, v_hbm, g_hbm,
     dq_ref, dk_ref, dv_ref,
-    qv, gv, gsend, hub_in, hub_out, gall, gpart, hub2_in, hub2_out, gall2,
+    owner_ref, lists_ref, goff_ref, small_sem, qv, gv, gsend, hub_in, hub_out, gall, gpart, hub2_in, cross_out, cross_in, hub2_out, gall2, cross_sem,
     keep_ex, keep_dp, keep_ds, wslot, own, sback, rback, load_sem, big_sem, ks_sem, kr_sem, gs_sem, gr_sem, hs_sem, hr_sem,
     *kvw,
 ):
     me = lax.axis_index("seq")
-    rpp = gtok // PIECE
-    pieces = 2 * heads * rpp
+    hubs = 2 * heads
     rows = nb * BLOCK
+    first = n // 2 - hubs + 1
+    hub = (me - first) // 2
+    col = lax.rem(me // 2, 2)
+    lane = (me // 4) * 2 + lax.rem(me, 2)
+    level = hub // 2
+    group_of = jnp.where(col == 0, level, heads - 1 - level)
+    other_hub = first + 2 * (hubs - 1 - hub)
+
+    def hub_id(g):
+        return first + jnp.where(col == 0, 4 * g, 4 * (heads - 1 - g) + 2)
+
+    def hubbed(i):
+        return (i >= first) & (i < first + 2 * hubs) & (lax.rem(i + first, 2) == 0)
+
+    barrier = pltpu.get_barrier_semaphore()
+
+    def greet(other):
+        pl.semaphore_signal(
+            barrier, inc=1, device_id={"seq": other}, device_id_type=pl.DeviceIdType.MESH
+        )
+
+    mine_hub = hubbed(me)
+
+    @pl.when(mine_hub)
+    def _():
+        @pl.loop(1, n)
+        def _(i):
+            greet(lax.rem(me + i, n))
+
+    @pl.when(~mine_hub)
+    def _():
+        @pl.when(me > 0)
+        def _():
+            greet(me - 1)
+
+        @pl.when(me < n - 1)
+        def _():
+            greet(me + 1)
+
     src_refs = (k_hbm, v_hbm)
-
     loads = []
     for t in range(2):
         for c in range(heads):
@@ -51,31 +87,23 @@
                 )
                 cp.start()
                 loads.append(cp)
+    small = [
+        pltpu.make_async_copy(a, b, small_sem.at[i])
+        for i, (a, b) in enumerate(
+            ((goff_hbm, goff_ref), (owner_hbm, owner_ref), (lists_hbm, lists_ref))
+        )
+    ]
+    for cp in small:
+        cp.start()
     cq = pltpu.make_async_copy(q_hbm.at[0], qv, big_sem.at[0])
     cg = pltpu.make_async_copy(g_hbm.at[0], gv, big_sem.at[1])
     cq.start()
     cg.start()
 
-    barrier = pltpu.get_barrier_semaphore()
-
-    first = (n - pieces) // 2
-    hub = me - first
-
-    def hubbed(i):
-        return (i >= first) & (i < first + pieces)
-
-    @pl.loop(1, n)
-    def _(i):
-        other = lax.rem(me + i, n)
-
-        @pl.when(hubbed(me) | hubbed(other) | (other == me + 1) | (other == me - 1))
-        def _():
-            pl.semaphore_signal(
-                barrier, inc=1, device_id={"seq": other}, device_id_type=pl.DeviceIdType.MESH
-            )
-
-    for cp in loads:
-        cp.wait()
+    with jax.named_scope("w_loads"):
+        small[0].wait()
+        for cp in loads:
+            cp.wait()
 
     hot = lax.broadcasted_iota(jnp.int32, (rows, gtok), 0) == goff_ref[...]
     hot = jnp.where(hot, 1.0, 0.0).astype(BF16)
@@ -83,8 +111,7 @@
         for c in range(heads):
             mine = kvw[t * heads + c][REACH : REACH + nb].reshape(rows, DH)
             got = lax.dot_general(hot, mine, (((0,), (0,)), ((), ())), preferred_element_type=F32)
-            base = (t * heads + c) * rpp
-            gsend[base : base + rpp] = got.astype(BF16).reshape(rpp, PIECE, DH)
+            gsend[t * heads + c] = got.astype(BF16)
     zeros_kv = jnp.zeros((REACH, BLOCK, DH), BF16)
 
     @pl.when(me == 0)
@@ -104,7 +131,8 @@
 
     below = jnp.where((me > 0) & ~hubbed(me - 1), 1, 0)
     above = jnp.where((me < n - 1) & ~hubbed(me + 1), 1, 0)
-    pl.semaphore_wait(barrier, jnp.where(hubbed(me), n - 1, pieces + below + above))
+    with jax.named_scope("w_barrier"):
+        pl.semaphore_wait(barrier, jnp.where(mine_hub, hubs - 1, hubs) + below + above)
 
     def remote(src, dst, s_sem, r_sem, target):
         return pltpu.make_async_remote_copy(
@@ -113,17 +141,19 @@
         )
 
     def hub_send(src, dst, s_sem, r_sem, j):
-        @pl.when(j != hub)
-        def _():
-            remote(src.at[j], dst.at[me], s_sem, r_sem, first + j).start()
+        @pl.when(me != first + 2 * j)
+        def _():
+            remote(src.at[j], dst.at[me], s_sem, r_sem, first + 2 * j).start()
 
     def drain(ref, count, sem):
         part = ref.at[pl.ds(0, count)]
         pltpu.make_async_copy(part, part, sem).wait()
 
-    @pl.loop(0, pieces)
-    def _(i):
-        hub_send(gsend, hub_in, hs_sem.at[0], hr_sem.at[0], lax.rem(me + i, pieces))
+    def hub_sends(src, dst, i):
+        for j in range(hubs):
+            hub_send(src, dst, hs_sem.at[i], hr_sem.at[i], j)
+
+    hub_sends(gsend, hub_in, 0)
 
     def halo(direction, c, t):
         idx = (direction * heads + c) * 2 + t
@@ -146,25 +176,64 @@
         cond = me < n - 1 if up else me > 0
         pl.when(cond)(what)
 
+    place = lax.rem(me, 4)
+
+    def far(d):
+        return place == (3 if d == 0 else 0)
+
+    def halo_start(c, d, late):
+        for t in range(2):
+            cond = (me < n - 1 if d == 0 else me > 0) & (far(d) if late else ~far(d))
+            pl.when(cond)(lambda t=t: halo(d, c, t).start())
+
+    held = mine_hub & (place == 1)
+
+    halo_start(0, 0, False)
+    halo_start(0, 1, False)
+    for c in range(1, heads):
+        halo_start(c, 1, False)
+        pl.when(~held)(functools.partial(halo_start, c, 0, False))
+
+    even = lax.rem(me, 2) == 0
+
+    def halo_wait(c, paired):
+        for d in range(2):
+            cond = (me > 0 if d == 0 else me < n - 1) & ((even if d == 1 else ~even) == paired)
+            for t in range(2):
+                pl.when(cond)(lambda d=d, t=t: halo(d, c, t).wait_recv())
+
+    with jax.named_scope("w_pair"):
+        halo_wait(0, True)
     for c in range(heads):
-        for t in range(2):
-            for d in range(2):
-                each(d, False, lambda d=d, c=c, t=t: halo(d, c, t).start())
-
-    @pl.when(hubbed(me))
+        for d in range(2):
+            halo_start(c, d, True)
+
+    for cp in small[1:]:
+        cp.wait()
+
+    def broadcast(src, dst, i):
+        @pl.loop(1, n)
+        def _(k):
+            remote(src, dst.at[hub], hs_sem.at[i], hr_sem.at[i], lax.rem(me + k, n)).start()
+
+    @pl.when(mine_hub)
     def _():
         hub_in[me] = gsend[hub]
-        drain(hub_in, n - 1, hr_sem.at[0])
+        with jax.named_scope("w_hub1"):
+            drain(hub_in, n - 1, hr_sem.at[0])
         pick = hub_in[owner_ref[0]]
         hub_out[...] = pick
         gall[hub] = pick
-
-        @pl.loop(1, n)
-        def _(i):
-            remote(hub_out, gall.at[hub], hs_sem.at[1], hr_sem.at[1], lax.rem(me + i, n)).start()
-
-    cq.wait()
-    cg.wait()
+        broadcast(hub_out, gall, 1)
+
+        @pl.when(held)
+        def _():
+            for c in range(1, heads):
+                halo_start(c, 0, False)
+
+    with jax.named_scope('w_qg'):
+        cq.wait()
+        cg.wait()
     scale = DH ** (-0.5)
     fold = scale * LOG2E
     local_idx = [
@@ -179,8 +248,7 @@
         return jnp.concatenate([kvw[t * heads + c][local_idx[b][l]] for l in range(listed)], axis=0)
 
     def global_rows(ref, t, c):
-        base = (t * heads + c) * rpp
-        return ref[base : base + rpp].reshape(gtok, DH)
+        return ref[t * heads + c]
 
     def columns(c):
         return [slice((c * group + i) * DH, (c * group + i + 1) * DH) for i in range(group)]
@@ -189,11 +257,25 @@
         rsl = slice(b * BLOCK, (b + 1) * BLOCK)
         return jnp.concatenate([ref[rsl, s] for s in columns(c)], axis=0)
 
+    def back_start(c):
+        for d in range(2):
+            each(d, False, lambda d=d: back(d, c).start())
+
+    def drain_hubs(ref, sem):
+        @pl.when(mine_hub)
+        def _():
+            drain(ref, hubs - 1, sem)
+
+        @pl.when(~mine_hub)
+        def _():
+            drain(ref, hubs, sem)
+
     stats = {}
     for c in range(heads):
-        for t in range(2):
-            for d in range(2):
-                each(d, True, lambda d=d, c=c, t=t: halo(d, c, t).wait_recv())
+        with jax.named_scope(f"w_halo{c}"):
+            if c > 0:
+                halo_wait(c, True)
+            halo_wait(c, False)
         for b in range(nb):
             st = nt(listed_rows(0, c, b), stacked(qv, c, b))
             dp = nt(listed_rows(1, c, b), stacked(gv, c, b))
@@ -206,16 +288,9 @@
                 jnp.sum(ex, axis=0, keepdims=True),
                 jnp.sum(ex * dp, axis=0, keepdims=True),
             )
-
-    @pl.when(hubbed(me))
-    def _():
-        drain(gall, pieces - 1, hr_sem.at[1])
-
-    @pl.when(~hubbed(me))
-    def _():
-        drain(gall, pieces, hr_sem.at[1])
-
-    for c in range(heads):
+        if c == 0:
+            with jax.named_scope("w_gall"):
+                drain_hubs(gall, hr_sem.at[1])
         kg, vg = global_rows(gall, 0, c), global_rows(gall, 1, c)
         glob = [None, None]
         for b in range(nb):
@@ -235,12 +310,14 @@
             for t, part in enumerate((nn(ds, qs) * scale, nn(pr.astype(BF16), gs))):
                 glob[t] = part if glob[t] is None else glob[t] + part
         for t in range(2):
-            base = (t * heads + c) * rpp
-            gpart[base : base + rpp] = glob[t].astype(BF16).reshape(rpp, PIECE, DH)
-
-    @pl.loop(0, pieces)
-    def _(i):
-        hub_send(gpart, hub2_in, hs_sem.at[2], hr_sem.at[2], lax.rem(me + i, pieces))
+            gpart[c, t] = glob[t].astype(BF16)
+
+    for g in range(heads):
+        @pl.when(me != hub_id(g))
+        def _():
+            remote(
+                gpart.at[g], hub2_in.at[lane], hs_sem.at[2], hr_sem.at[2], hub_id(g)
+            ).start()
 
     for c in range(heads):
         for b in range(nb):
@@ -274,33 +351,52 @@
                 own[c, dst - REACH] = total
             else:
                 sback[0, c, dst - REACH - nb] = total.astype(BF16)
-        for d in range(2):
-            each(d, False, lambda d=d, c=c: back(d, c).start())
-
-    @pl.when(hubbed(me))
-    def _():
-        hub2_in[me] = gpart[hub]
-        drain(hub2_in, n - 1, hr_sem.at[2])
-        total = jnp.sum(hub2_in[...].astype(F32), axis=0).astype(BF16)
+        with jax.named_scope(f"s_back{c}"):
+            for d in range(2):
+                each(d, False, lambda d=d, c=c: back(d, c).start())
+
+    @pl.when(mine_hub)
+    def _():
+        with jax.named_scope("w_hub2"):
+            drain(hub2_in, n // 2 - 1, hr_sem.at[2])
+        hub2_in[lane] = gpart[group_of]
+        half = jnp.sum(hub2_in[...].astype(F32), axis=0)
+        cross_out[...] = half.astype(BF16)
+        cross = remote(cross_out, cross_in, cross_sem.at[0], cross_sem.at[1], other_hub)
+        cross.start()
+        with jax.named_scope("w_cross"):
+            cross.wait_recv()
+        total = (half + cross_in[...].astype(F32)).astype(BF16)
         hub2_out[...] = total
-        gall2[hub] = total
-
-        @pl.loop(1, n)
-        def _(i):
-            remote(hub2_out, gall2.at[hub], hs_sem.at[3], hr_sem.at[3], lax.rem(me + i, n)).start()
-
-        drain(gall2, pieces - 1, hr_sem.at[3])
-
-    @pl.when(~hubbed(me))
-    def _():
-        drain(gall2, pieces, hr_sem.at[3])
+        gall2[group_of] = total
+
+        @pl.loop(1, n // 2)
+        def _(k):
+            q = lax.rem(lane + k, n // 2)
+            target = (q // 2) * 4 + col * 2 + lax.rem(q, 2)
+            remote(hub2_out, gall2.at[group_of], hs_sem.at[3], hr_sem.at[3], target).start()
+
+        cross.wait_send()
+
+    def drain_groups(ref, sem):
+        @pl.when(mine_hub)
+        def _():
+            drain(ref, heads - 1, sem)
+
+        @pl.when(~mine_hub)
+        def _():
+            drain(ref, heads, sem)
+
+    with jax.named_scope("w_gall2"):
+        drain_groups(gall2, hr_sem.at[3])
 
     flag = jnp.where(owner_ref[0] == me, 1.0, 0.0)
     for c in range(heads):
-        for d in range(2):
-            each(d, True, lambda d=d, c=c: back(d, c).wait_recv())
+        with jax.named_scope(f'w_back{c}'):
+            for d in range(2):
+                each(d, True, lambda d=d, c=c: back(d, c).wait_recv())
         for t, out in enumerate((dk_ref, dv_ref)):
-            extra = nn(hot, global_rows(gall2, t, c)) * flag
+            extra = nn(hot, gall2[c, t]) * flag
             for i in range(nb):
                 rsl = slice(i * BLOCK, (i + 1) * BLOCK)
                 total = own[c, i, t] + extra[rsl]
@@ -313,17 +409,13 @@
                 each(d, False, lambda d=d, c=c, t=t: halo(d, c, t).wait_send())
             each(d, False, lambda d=d, c=c: back(d, c).wait_send())
 
-    @pl.when(hubbed(me))
-    def _():
-        drain(gsend, pieces - 1, hs_sem.at[0])
-        drain(gpart, pieces - 1, hs_sem.at[2])
+    @pl.when(mine_hub)
+    def _():
         drain(hub_in, n - 1, hs_sem.at[1])
-        drain(hub2_in, n - 1, hs_sem.at[3])
-
-    @pl.when(~hubbed(me))
-    def _():
-        drain(gsend, pieces, hs_sem.at[0])
-        drain(gpart, pieces, hs_sem.at[2])
+        drain(hub2_in, n // 2 - 1, hs_sem.at[3])
+
+    drain_hubs(gsend, hs_sem.at[0])
+    drain_groups(gpart, hs_sem.at[2])
 
 
 def write_out(*refs):
@@ -347,28 +439,34 @@
         nb = rows // BLOCK
         listed = block_lists.shape[2]
         gtok = global_offset.shape[1]
-        pieces = 2 * heads * gtok // PIECE
+        hubs = 2 * heads
         wide = nb + 2 * REACH
-        assert nb == REACH and n >= pieces
+        assert nb == REACH and n % 8 == 0 and n >= 2 * hubs and heads % 2 == 0
         vm = pl.BlockSpec(memory_space=pltpu.VMEM)
-        sm = pl.BlockSpec(memory_space=pltpu.SMEM)
         hb = pl.BlockSpec(memory_space=pl.ANY)
         held = pl.pallas_call(
             functools.partial(kernel, n, heads, group, nb, listed, gtok),
             out_shape=tuple(pltpu.VMEM(a.shape, BF16) for a in (query, keys, values)),
-            in_specs=[sm, sm, vm, hb, hb, hb, hb],
+            in_specs=[hb] * 7,
             out_specs=(vm, vm, vm),
             scratch_shapes=[
+                pltpu.SMEM(owner.shape, jnp.int32),
+                pltpu.SMEM(block_lists.shape, jnp.int32),
+                pltpu.VMEM(global_offset.shape, jnp.int32),
+                pltpu.SemaphoreType.DMA((3,)),
                 pltpu.VMEM((rows, qw), BF16),
                 pltpu.VMEM((rows, qw), BF16),
-                pltpu.VMEM((pieces, PIECE, DH), BF16),
-                pltpu.VMEM((n, PIECE, DH), BF16),
-                pltpu.VMEM((PIECE, DH), BF16),
-                pltpu.VMEM((pieces, PIECE, DH), BF16),
-                pltpu.VMEM((pieces, PIECE, DH), BF16),
-                pltpu.VMEM((n, PIECE, DH), BF16),
-                pltpu.VMEM((PIECE, DH), BF16),
-                pltpu.VMEM((pieces, PIECE, DH), BF16),
+                pltpu.VMEM((hubs, gtok, DH), BF16),
+                pltpu.VMEM((n, gtok, DH), BF16),
+                pltpu.VMEM((gtok, DH), BF16),
+                pltpu.VMEM((hubs, gtok, DH), BF16),
+                pltpu.VMEM((heads, 2, gtok, DH), BF16),
+                pltpu.VMEM((n // 2, 2, gtok, DH), BF16),
+                pltpu.VMEM((2, gtok, DH), BF16),
+                pltpu.VMEM((2, gtok, DH), BF16),
+                pltpu.VMEM((2, gtok, DH), BF16),
+                pltpu.VMEM((heads, 2, gtok, DH), BF16),
+                pltpu.SemaphoreType.DMA((2,)),
                 pltpu.VMEM((heads, nb, listed * BLOCK, group * BLOCK), F32),
                 pltpu.VMEM((heads, nb, listed * BLOCK, group * BLOCK), F32),
                 pltpu.VMEM((heads, nb, gtok, group * BLOCK), BF16),

time: 28.2 us -> 26.8 us (0.950)
  Pallas kernels: 27.4 us -> 26 us
    pallas_call x1, Pallas kernels: 26.5 us -> 25.1 us  [local(): pl.pallas_call(functools.partial(kernel, n, heads, group, nb, listed, gto...]
where the time goes in v1:
time: 26.8 us; the launch traced here: 26.6 us
  Pallas kernels  26 us (97%)
  between operations  0.64 us (2%)
    pallas_call x1, Pallas kernels, local(): pl.pallas_call(functools.partial(kernel, n, heads, group, nb, listed, gto...  25.1 us
    pallas_call x1, Pallas kernels, local(): pl.pallas_call(write_out, out_shape=tuple((jax.ShapeDtypeStruct(a.shape,...  0.9 us

profile of v1, /device:TPU:0, one launch (start us, length us, event | category | flops | bytes accessed | tf_op | source)
XLA Modules:
  0.0 26.6 jit_solution(167336529700949098)
XLA Ops:
  0.6 25.1 %shard_map.94 = (bf16[1,256,1024]{2,1,0:T(8,128)(2,1)S(1)}, bf16[1,256,256]{2,1,0:T(8,128)(2,1)S(1)}, bf16[1,256,256]{2,1,0:T(8,128)(2,1)S(1)}) custom-call(s32[16]{0:T(128)} %owner_hbm.1, s32[1,2,3]{2,1,0:T(2,128)} %lists_hbm.1, s32[1,64]{1,0:T(1,128)} %goff_hbm.1, bf16[1,256,1024]{2,1,0:T(8,128)(2,1)} %q_hbm.1, bf16[1,256,256]{2,1,0:T(8,128)(2,1)} %k_hbm.1, ...), custom_call_target="tpu_custom_call" | custom-call | tf_op jit(solution)/shard_map/pallas_call | solution.py:447
  25.7 0.9 %shard_map.95 = (bf16[1,256,1024]{2,1,0:T(8,128)(2,1)}, bf16[1,256,256]{2,1,0:T(8,128)(2,1)}, bf16[1,256,256]{2,1,0:T(8,128)(2,1)}) custom-call(bf16[1,256,1024]{2,1,0:T(8,128)(2,1)S(1)} %get-tuple-element.6.refs_0_, bf16[1,256,256]{2,1,0:T(8,128)(2,1)S(1)} %get-tuple-element.7.refs_1_, bf16[1,256,256]{2,1,0:T(8,128)(2,1)S(1)} %get-tuple-element.8.refs_2_), custom_call_target="tpu_custom_call" | custom-call | tf_op jit(solution)/shard_map/pallas_call | solution.py:489

commit v2 on v1

v2 whole, which is shorter than its diff:
```python
import functools

import jax
import jax.numpy as jnp
from jax import lax
from jax.experimental import pallas as pl
from jax.experimental.pallas import tpu as pltpu
from jax.sharding import PartitionSpec as P

HQ = 16
HK = 4
DH = 128
BLOCK = 128
REACH = 2
LOG2E = 1.4426950408889634
F32 = jnp.float32
BF16 = jnp.bfloat16


def nt(a, b):
    return lax.dot_general(a, b, (((1,), (1,)), ((), ())), preferred_element_type=F32)


def nn(a, b):
    return lax.dot_general(a, b, (((1,), (0,)), ((), ())), preferred_element_type=F32)


def kernel(
    n, heads, group, nb, listed, gtok,
    owner_hbm, lists_hbm, goff_hbm, q_hbm, k_hbm, v_hbm, g_hbm,
    dq_ref, dk_ref, dv_ref,
    owner_ref, lists_ref, goff_ref, small_sem, qv, gv, gsend, hub_in, hub_out, gcand, gall, fw_sem, gpart, hub2_in, cross_out, cross_in, hub2_out, gall2, cross_sem,
    keep_ex, keep_dp, keep_ds, wslot, own, sback, rback, load_sem, big_sem, ks_sem, kr_sem, gs_sem, gr_sem, hs_sem, hr_sem,
    *kvw,
):
    me = lax.axis_index("seq")
    hubs = 2 * heads
    rows = nb * BLOCK
    first = n // 2 - hubs + 1
    hub = (me - first) // 2
    col = lax.rem(me // 2, 2)
    lane = (me // 4) * 2 + lax.rem(me, 2)
    odd = lax.rem(me, 2) == 1
    level = hub // 2
    group_of = jnp.where(col == 0, level, heads - 1 - level)

    def row_of(g, side):
        return jnp.where(side == 0, g, heads - 1 - g)

    def hub_id(g, side):
        return first + 4 * row_of(g, side) + 2 * side

    def sum_id(g, side):
        return 4 * (g + side) + 2 * side + 1

    def is_adder(i):
        g = i // 4 - lax.rem(i // 2, 2)
        return (g >= 0) & (g < heads) & (lax.rem(i, 2) == 1)

    adder = is_adder(me)
    sum_group = jnp.clip(me // 4 - col, 0, heads - 1)
    other_sum = sum_id(sum_group, 1 - col)

    def hubbed(i):
        return (i >= first) & (i < first + 2 * hubs) & (lax.rem(i + first, 2) == 0)

    src_refs = (k_hbm, v_hbm)
    loads = []
    for t in range(2):
        for c in range(heads):
            for i in range(nb):
                cp = pltpu.make_async_copy(
                    src_refs[t].at[0, pl.ds(i * BLOCK, BLOCK), pl.ds(c * DH, DH)],
                    kvw[t * heads + c].at[REACH + i],
                    load_sem.at[(t * heads + c) * nb + i],
                )
                cp.start()
                loads.append(cp)
    small = [
        pltpu.make_async_copy(a, b, small_sem.at[i])
        for i, (a, b) in enumerate(
            ((goff_hbm, goff_ref), (owner_hbm, owner_ref), (lists_hbm, lists_ref))
        )
    ]
    for cp in small:
        cp.start()

    barrier = pltpu.get_barrier_semaphore()

    def greet(other):
        pl.semaphore_signal(
            barrier, inc=1, device_id={"seq": other}, device_id_type=pl.DeviceIdType.MESH
        )

    mine_hub = hubbed(me)

    @pl.when(mine_hub | adder)
    def _():
        @pl.loop(0, n // 2)
        def _(k):
            target = (k // 2) * 4 + col * 2 + lax.rem(k, 2)

            @pl.when((target != me) & (target != me - 1))
            def _():
                greet(target)

    @pl.when(odd)
    def _():
        for g in range(heads):
            greet(hub_id(g, 1 - col))

    @pl.when(adder & ~hubbed(other_sum))
    def _():
        greet(other_sum)

    @pl.when(me > 0)
    def _():
        greet(me - 1)

    @pl.when(me < n - 1)
    def _():
        greet(me + 1)

    cq = pltpu.make_async_copy(q_hbm.at[0], qv, big_sem.at[0])
    cg = pltpu.make_async_copy(g_hbm.at[0], gv, big_sem.at[1])

    with jax.named_scope("w_loads"):
        small[0].wait()
        for cp in loads:
            cp.wait()
    cq.start()
    cg.start()

    hot = lax.broadcasted_iota(jnp.int32, (rows, gtok), 0) == goff_ref[...]
    hot = jnp.where(hot, 1.0, 0.0).astype(BF16)
    for t in range(2):
        for c in range(heads):
            mine = kvw[t * heads + c][REACH : REACH + nb].reshape(rows, DH)
            got = lax.dot_general(hot, mine, (((0,), (0,)), ((), ())), preferred_element_type=F32)
            gsend[c, t] = got.astype(BF16)
    zeros_kv = jnp.zeros((REACH, BLOCK, DH), BF16)

    @pl.when(me == 0)
    def _():
        for ref in kvw:
            ref[0:REACH] = zeros_kv
        rback[0] = jnp.zeros(rback.shape[1:], BF16)

    @pl.when(me == n - 1)
    def _():
        for ref in kvw:
            ref[REACH + nb : REACH + nb + REACH] = zeros_kv
        rback[1] = jnp.zeros(rback.shape[1:], BF16)

    zero_tile = jnp.zeros((nb, 2, BLOCK, DH), F32)
    wslot[:, listed] = zero_tile

    def served(i):
        return jnp.where(hubbed(i) | is_adder(i), 1, 0)

    beside = jnp.where(me > 0, 1, 0) + jnp.where(me < n - 1, 1, 0)
    callers = sum(
        jnp.where(is_adder(hub_id(g, col)), 0, 1) for g in range(heads)
    ) + heads
    greeted = callers - served(me) - jnp.where(odd, 0, served(me + 1))
    greeted = greeted + jnp.where(mine_hub, n // 4, 0) + jnp.where(adder & ~mine_hub, 1, 0)
    with jax.named_scope("w_barrier"):
        pl.semaphore_wait(barrier, beside + greeted)

    def remote(src, dst, s_sem, r_sem, target):
        return pltpu.make_async_remote_copy(
            src_ref=src, dst_ref=dst, send_sem=s_sem, recv_sem=r_sem,
            device_id={"seq": target}, device_id_type=pl.DeviceIdType.MESH,
        )

    def to_hub(src, dst, i, g, target):
        @pl.when(me != target)
        def _():
            remote(src.at[g], dst.at[lane], hs_sem.at[i], hr_sem.at[i], target).start()

    def drain(ref, count, sem):
        part = ref.at[pl.ds(0, count)]
        pltpu.make_async_copy(part, part, sem).wait()

    for g in range(heads):
        to_hub(gsend, hub_in, 0, g, hub_id(g, col))

    def halo(direction, c, t):
        idx = (direction * heads + c) * 2 + t
        ref = kvw[t * heads + c]
        if direction == 0:
            src, dst, target = ref.at[pl.ds(nb, REACH)], ref.at[pl.ds(0, REACH)], me + 1
        else:
            src, dst, target = ref.at[pl.ds(REACH, REACH)], ref.at[pl.ds(REACH + nb, REACH)], me - 1
        return remote(src, dst, ks_sem.at[idx], kr_sem.at[idx], target)

    def back(direction, c):
        idx = direction * heads + c
        target = me + 1 if direction == 0 else me - 1
        return remote(
            sback.at[direction, c], rback.at[direction, c], gs_sem.at[idx], gr_sem.at[idx], target
        )

    def each(direction, receiving, what):
        up = (direction == 0) != receiving
        cond = me < n - 1 if up else me > 0
        pl.when(cond)(what)

    place = lax.rem(me, 4)

    def far(d):
        return place == (3 if d == 0 else 0)

    def halo_start(c, d, late):
        for t in range(2):
            cond = (me < n - 1 if d == 0 else me > 0) & (far(d) if late else ~far(d))
            pl.when(cond)(lambda t=t: halo(d, c, t).start())

    held = mine_hub & (place == 1)

    halo_start(0, 0, False)
    halo_start(0, 1, False)
    for c in range(1, heads):
        halo_start(c, 1, False)
        pl.when(~held)(functools.partial(halo_start, c, 0, False))
    for c in range(heads):
        for d in range(2):
            halo_start(c, d, True)

    def halo_wait(c, paired):
        for d in range(2):
            cond = (me > 0 if d == 0 else me < n - 1) & ((odd if d == 0 else ~odd) == paired)
            for t in range(2):
                pl.when(cond)(lambda d=d, t=t: halo(d, c, t).wait_recv())

    for cp in small[1:]:
        cp.wait()

    with jax.named_scope('w_qg'):
        cq.wait()
        cg.wait()
    scale = DH ** (-0.5)
    fold = scale * LOG2E
    local_idx = [
        [
            jnp.clip(lists_ref[0, b, l] - me * nb + REACH, 0, nb + 2 * REACH - 1)
            for l in range(listed)
        ]
        for b in range(nb)
    ]

    def near_rows(t, c, b):
        return [kvw[t * heads + c][local_idx[b][l]] for l in range(1, listed)]

    def columns(c):
        return [slice((c * group + i) * DH, (c * group + i + 1) * DH) for i in range(group)]

    def stacked(ref, c, b):
        rsl = slice(b * BLOCK, (b + 1) * BLOCK)
        return jnp.concatenate([ref[rsl, s] for s in columns(c)], axis=0)

    def logits(ks, vs, c, b):
        return nt(ks, stacked(qv, c, b)), nt(vs, stacked(gv, c, b))

    def keep(c, b, start, st, dp):
        top = jnp.max(st, axis=0, keepdims=True)
        ex = jnp.exp2((st - top) * fold)
        keep_ex[c, b, start : start + st.shape[0]] = ex
        keep_dp[c, b, start : start + st.shape[0]] = dp
        total = jnp.sum(ex, axis=0, keepdims=True)
        return top, total, jnp.sum(ex * dp, axis=0, keepdims=True)

    window = listed * BLOCK
    stats = {}
    for c in range(heads):
        for b in range(nb):
            kb, vb = kvw[c][REACH + b], kvw[heads + c][REACH + b]
            stats[c, b] = [keep(c, b, 0, *logits(kb, vb, c, b))]

    def far_first(i, count):
        return jnp.where(lax.rem(i, 2) == 0, count - 1 - i // 2, i // 2)

    owner_at = owner_ref[0]

    @pl.when(mine_hub)
    def _():
        with jax.named_scope("w_hub1"):
            drain(hub_in, n // 2 - 1, hr_sem.at[0])
        hub_in[lane] = gsend[group_of]
        pick = hub_in[(owner_at // 4) * 2 + lax.rem(owner_at, 2)]
        hub_out[...] = pick
        gcand[col * heads + group_of] = pick

        @pl.loop(0, n // 2)
        def _(k):
            target = 4 * far_first(k // 2, n // 4) + 2 * lax.rem(k, 2) + 1

            @pl.when(target != me)
            def _():
                remote(
                    hub_out, gcand.at[col * heads + group_of], hs_sem.at[1], hr_sem.at[1], target
                ).start()

        @pl.when(held)
        def _():
            for c in range(1, heads):
                halo_start(c, 0, False)

    def back_start(c):
        for d in range(2):
            each(d, False, lambda d=d: back(d, c).start())

    def drain_own(ref, count, sem, self_served):
        @pl.when(self_served)
        def _():
            drain(ref, count - 1, sem)

        @pl.when(~self_served)
        def _():
            drain(ref, count, sem)

    pass_on = remote(gall, gall, fw_sem.at[0], fw_sem.at[1], jnp.where(odd, me - 1, me + 1))

    def collect():
        with jax.named_scope("w_cand"):
            drain_own(gcand, 2 * heads, hr_sem.at[1], mine_hub)
        side = lax.rem(owner_at // 2, 2) * heads
        for g in range(heads):
            gall[g] = gcand[side + g]
        pass_on.start()

    ratios = {}
    for c in range(heads):
        last = c == heads - 1
        with jax.named_scope(f"w_halo{c}"):
            halo_wait(c, True)
            halo_wait(c, False)
        if not last:
            for b in range(nb):
                kn = jnp.concatenate(near_rows(0, c, b), axis=0)
                vn = jnp.concatenate(near_rows(1, c, b), axis=0)
                stats[c, b].append(keep(c, b, BLOCK, *logits(kn, vn, c, b)))
        if c == 0:
            pl.when(odd)(collect)
            with jax.named_scope("w_gall"):
                @pl.when(~odd)
                def _():
                    pass_on.wait_recv()
        glob = [None, None]
        for b in range(nb):
            qs, gs = stacked(qv, c, b), stacked(gv, c, b)
            kn, vn = [gall[c, 0]], [gall[c, 1]]
            if last:
                kn, vn = near_rows(0, c, b) + kn, near_rows(1, c, b) + vn
            st, dp = logits(jnp.concatenate(kn, axis=0), jnp.concatenate(vn, axis=0), c, b)
            top = jnp.max(st, axis=0, keepdims=True)
            for old in stats[c, b]:
                top = jnp.maximum(top, old[0])
            ex = jnp.exp2((st - top) * fold)
            total = jnp.sum(ex, axis=0, keepdims=True)
            dot = jnp.sum(ex * dp, axis=0, keepdims=True)
            shrinks = [jnp.exp2((old[0] - top) * fold) for old in stats[c, b]]
            for shrink, old in zip(shrinks, stats[c, b]):
                total = total + old[1] * shrink
                dot = dot + old[2] * shrink
            inv = 1.0 / total
            dot = dot * inv
            if last:
                near = window - BLOCK
                keep_ex[c, b, BLOCK:window] = ex[:near]
                keep_dp[c, b, BLOCK:window] = dp[:near]
                ex, dp = ex[near:], dp[near:]
            pr = ex * inv
            ds = (pr * (dp - dot)).astype(BF16)
            keep_ds[c, b, window:] = ds
            own_ratio = shrinks[0] * inv
            ratios[c, b] = (own_ratio, inv if last else shrinks[1] * inv, dot)
            for t, part in enumerate((nn(ds, qs) * scale, nn(pr.astype(BF16), gs))):
                glob[t] = part if glob[t] is None else glob[t] + part
        for t in range(2):
            gpart[c, t] = glob[t].astype(BF16)
        with jax.named_scope(f"s_gpart{c}"):
            to_hub(gpart, hub2_in, 2, c, sum_id(c, col))

    for c in range(heads):
        for b in range(nb):
            qs, gs = stacked(qv, c, b), stacked(gv, c, b)
            own_ratio, near_ratio, dot = ratios[c, b]
            vals = []
            for lo, hi, ratio in ((0, BLOCK, own_ratio), (BLOCK, window, near_ratio)):
                pr = keep_ex[c, b, lo:hi] * ratio
                ds = (pr * (keep_dp[c, b, lo:hi] - dot)).astype(BF16)
                keep_ds[c, b, lo:hi] = ds
                vals.append((ds, pr.astype(BF16)))
            ds, pr = (jnp.concatenate([v[i] for v in vals], axis=0) for i in range(2))
            for t, val in enumerate((nn(ds, qs) * scale, nn(pr, gs))):
                for l in range(listed):
                    wslot[b, l, t] = val[l * BLOCK : (l + 1) * BLOCK]
        for dst in range(nb + 2 * REACH):
            total = None
            for b in range(nb):
                if not b <= dst <= b + 2 * REACH:
                    continue
                slot = jnp.int32(listed)
                for l in range(1, listed):
                    slot = jnp.where(local_idx[b][l] == dst, l, slot)
                term = wslot[b, 0] if dst == b + REACH else wslot[b, slot]
                total = term if total is None else total + term
            if dst < REACH:
                sback[1, c, dst] = total.astype(BF16)
            elif dst < REACH + nb:
                own[c, dst - REACH] = total
            else:
                sback[0, c, dst - REACH - nb] = total.astype(BF16)
        with jax.named_scope(f"s_back{c}"):
            back_start(c)

    for c in range(heads):
        for b in range(nb):
            ks = jnp.concatenate([kvw[c][REACH + b]] + near_rows(0, c, b) + [gall[c, 0]], axis=0)
            dqt = nn(ks.T, keep_ds[c, b]) * scale
            dq = dqt.T.astype(BF16)
            for i, s in enumerate(columns(c)):
                dq_ref[0, b * BLOCK : (b + 1) * BLOCK, s] = dq[i * BLOCK : (i + 1) * BLOCK]

    @pl.when(adder)
    def _():
        with jax.named_scope("w_hub2"):
            drain(hub2_in, n // 2 - 1, hr_sem.at[2])
        hub2_in[lane] = gpart[sum_group]
        half = jnp.sum(hub2_in[...].astype(F32), axis=0)
        cross_out[...] = half.astype(BF16)
        cross = remote(cross_out, cross_in, cross_sem.at[0], cross_sem.at[1], other_sum)
        cross.start()
        with jax.named_scope("w_cross"):
            cross.wait_recv()
        total = (half + cross_in[...].astype(F32)).astype(BF16)
        hub2_out[...] = total
        gall2[sum_group] = total

        @pl.loop(0, n // 2)
        def _(k):
            target = 4 * far_first(k // 2, n // 4) + col * 2 + lax.rem(k, 2)

            @pl.when(target != me)
            def _():
                remote(
                    hub2_out, gall2.at[sum_group], hs_sem.at[3], hr_sem.at[3], target
                ).start()

        cross.wait_send()

    for c in range(heads):
        with jax.named_scope(f"w_back{c}"):
            for d in range(2):
                each(d, True, lambda d=d, c=c: back(d, c).wait_recv())
        for t in range(2):
            for i in range(nb):
                total = rback[0, c, i, t].astype(F32) + rback[1, c, i, t].astype(F32)
                own[c, i, t] = own[c, i, t] + total

    with jax.named_scope("w_gall2"):
        drain_own(gall2, heads, hr_sem.at[3], adder)

    flag = jnp.where(owner_ref[0] == me, 1.0, 0.0)
    for c in range(heads):
        for t, out in enumerate((dk_ref, dv_ref)):
            extra = nn(hot, gall2[c, t]) * flag
            for i in range(nb):
                rsl = slice(i * BLOCK, (i + 1) * BLOCK)
                out[0, rsl, c * DH : (c + 1) * DH] = (own[c, i, t] + extra[rsl]).astype(BF16)

    for c in range(heads):
        for d in range(2):
            for t in range(2):
                each(d, False, lambda d=d, c=c, t=t: halo(d, c, t).wait_send())
            each(d, False, lambda d=d, c=c: back(d, c).wait_send())

    @pl.when(odd)
    def _():
        pass_on.wait_send()

    @pl.when(mine_hub)
    def _():
        drain(hub_in, n // 2 - 1, hs_sem.at[1])

    @pl.when(adder)
    def _():
        drain(hub2_in, n // 2 - 1, hs_sem.at[3])

    drain_own(gsend, heads, hs_sem.at[0], mine_hub)
    drain_own(gpart, heads, hs_sem.at[2], adder)


def write_out(*refs):
    copies = [
        pltpu.make_async_copy(refs[i], refs[3 + i], refs[6].at[i]) for i in range(3)
    ]
    for cp in copies:
        cp.start()
    for cp in copies:
        cp.wait()


def solution(mesh):
    n = mesh.shape["seq"]

    def local(query, keys, values, grad_out, global_offset, owner, block_lists):
        rows, qw = query.shape[1:]
        kw = keys.shape[2]
        heads = kw // DH
        group = HQ // HK
        nb = rows // BLOCK
        listed = block_lists.shape[2]
        gtok = global_offset.shape[1]
        hubs = 2 * heads
        wide = nb + 2 * REACH
        assert nb == REACH and n % 8 == 0 and n >= 2 * hubs and heads % 2 == 0
        vm = pl.BlockSpec(memory_space=pltpu.VMEM)
        hb = pl.BlockSpec(memory_space=pl.ANY)
        held = pl.pallas_call(
            functools.partial(kernel, n, heads, group, nb, listed, gtok),
            out_shape=tuple(pltpu.VMEM(a.shape, BF16) for a in (query, keys, values)),
            in_specs=[hb] * 7,
            out_specs=(vm, vm, vm),
            scratch_shapes=[
                pltpu.SMEM(owner.shape, jnp.int32),
                pltpu.SMEM(block_lists.shape, jnp.int32),
                pltpu.VMEM(global_offset.shape, jnp.int32),
                pltpu.SemaphoreType.DMA((3,)),
                pltpu.VMEM((rows, qw), BF16),
                pltpu.VMEM((rows, qw), BF16),
                pltpu.VMEM((heads, 2, gtok, DH), BF16),
                pltpu.VMEM((n // 2, 2, gtok, DH), BF16),
                pltpu.VMEM((2, gtok, DH), BF16),
                pltpu.VMEM((2 * heads, 2, gtok, DH), BF16),
                pltpu.VMEM((heads, 2, gtok, DH), BF16),
                pltpu.SemaphoreType.DMA((2,)),
                pltpu.VMEM((heads, 2, gtok, DH), BF16),
                pltpu.VMEM((n // 2, 2, gtok, DH), BF16),
                pltpu.VMEM((2, gtok, DH), BF16),
                pltpu.VMEM((2, gtok, DH), BF16),
                pltpu.VMEM((2, gtok, DH), BF16),
                pltpu.VMEM((heads, 2, gtok, DH), BF16),
                pltpu.SemaphoreType.DMA((2,)),
                pltpu.VMEM((heads, nb, listed * BLOCK, group * BLOCK), F32),
                pltpu.VMEM((heads, nb, listed * BLOCK, group * BLOCK), F32),
                pltpu.VMEM((heads, nb, listed * BLOCK + gtok, group * BLOCK), BF16),
                pltpu.VMEM((nb, listed + 1, 2, BLOCK, DH), F32),
                pltpu.VMEM((heads, nb, 2, BLOCK, DH), F32),
                pltpu.VMEM((2, heads, REACH, 2, BLOCK, DH), BF16),
                pltpu.VMEM((2, heads, REACH, 2, BLOCK, DH), BF16),
                pltpu.SemaphoreType.DMA((2 * heads * nb,)),
                pltpu.SemaphoreType.DMA((2,)),
                pltpu.SemaphoreType.DMA((4 * heads,)),
                pltpu.SemaphoreType.DMA((4 * heads,)),
                pltpu.SemaphoreType.DMA((2 * heads,)),
                pltpu.SemaphoreType.DMA((2 * heads,)),
                pltpu.SemaphoreType.DMA((4,)),
                pltpu.SemaphoreType.DMA((4,)),
            ]
            + [pltpu.VMEM((wide, BLOCK, DH), BF16)] * (2 * heads),
            compiler_params=pltpu.CompilerParams(collective_id=0, has_side_effects=True),
        )(owner, block_lists, global_offset, query, keys, values, grad_out)
        return pl.pallas_call(
            write_out,
            out_shape=tuple(jax.ShapeDtypeStruct(a.shape, BF16) for a in (query, keys, values)),
            in_specs=[hb] * 3,
            out_specs=[hb] * 3,
            scratch_shapes=[pltpu.SemaphoreType.DMA((3,))],
        )(*[pltpu.with_memory_space_constraint(a, pltpu.VMEM) for a in held])

    return jax.shard_map(
        local,
        mesh=mesh,
        in_specs=(
            P(None, "seq", "head"),
            P(None, "seq", "head"),
            P(None, "seq", "head"),
            P(None, "seq", "head"),
            P(),
            P(),
            P(None, "seq", None),
        ),
        out_specs=(P(None, "seq", "head"), P(None, "seq", "head"), P(None, "seq", "head")),
        check_vma=False,
    )
```

time: 26.8 us -> 25.9 us (0.966)
  Pallas kernels: 26 us -> 25 us
    pallas_call x1, Pallas kernels: 25.1 us -> 24.1 us  [local(): pl.pallas_call(functools.partial(kernel, n, heads, group, nb, listed, gto...]
where the time goes in v2:
time: 25.9 us; the launch traced here: 25.7 us
  Pallas kernels  25 us (97%)
  between operations  0.64 us (2%)
    pallas_call x1, Pallas kernels, local(): pl.pallas_call(functools.partial(kernel, n, heads, group, nb, listed, gto...  24.1 us
    pallas_call x1, Pallas kernels, local(): pl.pallas_call(write_out, out_shape=tuple((jax.ShapeDtypeStruct(a.shape,...  0.9 us

profile of v2, /device:TPU:0, one launch (start us, length us, event | category | flops | bytes accessed | tf_op | source)
XLA Modules:
  0.0 25.7 jit_solution(8040069415709223606)
XLA Ops:
  0.6 24.1 %shard_map.94 = (bf16[1,256,1024]{2,1,0:T(8,128)(2,1)S(1)}, bf16[1,256,256]{2,1,0:T(8,128)(2,1)S(1)}, bf16[1,256,256]{2,1,0:T(8,128)(2,1)S(1)}) custom-call(s32[16]{0:T(128)} %owner_hbm.1, s32[1,2,3]{2,1,0:T(2,128)} %lists_hbm.1, s32[1,64]{1,0:T(1,128)} %goff_hbm.1, bf16[1,256,1024]{2,1,0:T(8,128)(2,1)} %q_hbm.1, bf16[1,256,256]{2,1,0:T(8,128)(2,1)} %k_hbm.1, ...), custom_call_target="tpu_custom_call" | custom-call | tf_op jit(solution)/shard_map/pallas_call | solution.py:521
  24.8 0.9 %shard_map.95 = (bf16[1,256,1024]{2,1,0:T(8,128)(2,1)}, bf16[1,256,256]{2,1,0:T(8,128)(2,1)}, bf16[1,256,256]{2,1,0:T(8,128)(2,1)}) custom-call(bf16[1,256,1024]{2,1,0:T(8,128)(2,1)S(1)} %get-tuple-element.6.refs_0_, bf16[1,256,256]{2,1,0:T(8,128)(2,1)S(1)} %get-tuple-element.7.refs_1_, bf16[1,256,256]{2,1,0:T(8,128)(2,1)S(1)} %get-tuple-element.8.refs_2_), custom_call_target="tpu_custom_call" | custom-call | tf_op jit(solution)/shard_map/pallas_call | solution.py:565

commit v3 on v2

--- a/solution.py
+++ b/solution.py
@@ -12,6 +12,7 @@
 DH = 128
 BLOCK = 128
 REACH = 2
+LEADS = 2
 LOG2E = 1.4426950408889634
 F32 = jnp.float32
 BF16 = jnp.bfloat16
@@ -29,7 +30,7 @@
     n, heads, group, nb, listed, gtok,
     owner_hbm, lists_hbm, goff_hbm, q_hbm, k_hbm, v_hbm, g_hbm,
     dq_ref, dk_ref, dv_ref,
-    owner_ref, lists_ref, goff_ref, small_sem, qv, gv, gsend, hub_in, hub_out, gcand, gall, fw_sem, gpart, hub2_in, cross_out, cross_in, hub2_out, gall2, cross_sem,
+    owner_ref, lists_ref, goff_ref, small_sem, qv, gv, gsend, hub_in, hub_out, gcand, gall, fw_sem, gpart, hub2_in, half_out, total_out, cross_in, sums, cross_sem,
     keep_ex, keep_dp, keep_ds, wslot, own, sback, rback, load_sem, big_sem, ks_sem, kr_sem, gs_sem, gr_sem, hs_sem, hr_sem,
     *kvw,
 ):
@@ -94,7 +95,7 @@
 
     mine_hub = hubbed(me)
 
-    @pl.when(mine_hub | adder)
+    @pl.when(mine_hub)
     def _():
         @pl.loop(0, n // 2)
         def _(k):
@@ -108,10 +109,6 @@
     def _():
         for g in range(heads):
             greet(hub_id(g, 1 - col))
-
-    @pl.when(adder & ~hubbed(other_sum))
-    def _():
-        greet(other_sum)
 
     @pl.when(me > 0)
     def _():
@@ -152,18 +149,18 @@
             ref[REACH + nb : REACH + nb + REACH] = zeros_kv
         rback[1] = jnp.zeros(rback.shape[1:], BF16)
 
+    lead = me < LEADS
+    no_sum = jnp.zeros((2, gtok, DH), BF16)
+    for g in range(heads):
+        @pl.when(~lead | (adder & (sum_group == g)))
+        def _():
+            sums[heads + g] = no_sum
+
     zero_tile = jnp.zeros((nb, 2, BLOCK, DH), F32)
     wslot[:, listed] = zero_tile
 
-    def served(i):
-        return jnp.where(hubbed(i) | is_adder(i), 1, 0)
-
     beside = jnp.where(me > 0, 1, 0) + jnp.where(me < n - 1, 1, 0)
-    callers = sum(
-        jnp.where(is_adder(hub_id(g, col)), 0, 1) for g in range(heads)
-    ) + heads
-    greeted = callers - served(me) - jnp.where(odd, 0, served(me + 1))
-    greeted = greeted + jnp.where(mine_hub, n // 4, 0) + jnp.where(adder & ~mine_hub, 1, 0)
+    greeted = heads + jnp.where(mine_hub, n // 4 - 1, 0) - jnp.where(hubbed(me + 1), 1, 0)
     with jax.named_scope("w_barrier"):
         pl.semaphore_wait(barrier, beside + greeted)
 
@@ -423,30 +420,36 @@
             for i, s in enumerate(columns(c)):
                 dq_ref[0, b * BLOCK : (b + 1) * BLOCK, s] = dq[i * BLOCK : (i + 1) * BLOCK]
 
+    def give(src, target, at):
+        remote(src, sums.at[at], hs_sem.at[3], hr_sem.at[3], target).start()
+
     @pl.when(adder)
     def _():
         with jax.named_scope("w_hub2"):
             drain(hub2_in, n // 2 - 1, hr_sem.at[2])
         hub2_in[lane] = gpart[sum_group]
         half = jnp.sum(hub2_in[...].astype(F32), axis=0)
-        cross_out[...] = half.astype(BF16)
-        cross = remote(cross_out, cross_in, cross_sem.at[0], cross_sem.at[1], other_sum)
+        half_out[...] = half.astype(BF16)
+        cross = remote(half_out, cross_in, cross_sem.at[0], cross_sem.at[1], other_sum)
         cross.start()
+        for target in range(LEADS):
+            @pl.when((me != target) & (other_sum != target))
+            def _():
+                give(half_out, target, col * heads + sum_group)
+
         with jax.named_scope("w_cross"):
             cross.wait_recv()
         total = (half + cross_in[...].astype(F32)).astype(BF16)
-        hub2_out[...] = total
-        gall2[sum_group] = total
+        total_out[...] = total
+        sums[sum_group] = total
 
         @pl.loop(0, n // 2)
         def _(k):
             target = 4 * far_first(k // 2, n // 4) + col * 2 + lax.rem(k, 2)
 
-            @pl.when(target != me)
+            @pl.when((target != me) & (target >= LEADS))
             def _():
-                remote(
-                    hub2_out, gall2.at[sum_group], hs_sem.at[3], hr_sem.at[3], target
-                ).start()
+                give(total_out, target, sum_group)
 
         cross.wait_send()
 
@@ -459,16 +462,8 @@
                 total = rback[0, c, i, t].astype(F32) + rback[1, c, i, t].astype(F32)
                 own[c, i, t] = own[c, i, t] + total
 
-    with jax.named_scope("w_gall2"):
-        drain_own(gall2, heads, hr_sem.at[3], adder)
-
     flag = jnp.where(owner_ref[0] == me, 1.0, 0.0)
-    for c in range(heads):
-        for t, out in enumerate((dk_ref, dv_ref)):
-            extra = nn(hot, gall2[c, t]) * flag
-            for i in range(nb):
-                rsl = slice(i * BLOCK, (i + 1) * BLOCK)
-                out[0, rsl, c * DH : (c + 1) * DH] = (own[c, i, t] + extra[rsl]).astype(BF16)
+    hot_twice = (jnp.concatenate([hot, hot], axis=1).astype(F32) * flag).astype(BF16)
 
     for c in range(heads):
         for d in range(2):
@@ -488,8 +483,28 @@
     def _():
         drain(hub2_in, n // 2 - 1, hs_sem.at[3])
 
+    for extra_sends in (1, LEADS):
+        @pl.when(adder & (col == 1) & ((other_sum < LEADS) == (extra_sends < LEADS)))
+        def _():
+            drain(hub2_in, extra_sends, hs_sem.at[3])
+
     drain_own(gsend, heads, hs_sem.at[0], mine_hub)
     drain_own(gpart, heads, hs_sem.at[2], adder)
+
+    with jax.named_scope("w_gall2"):
+        for is_adder_too in range(2):
+            for leads in range(2):
+                @pl.when((adder if is_adder_too else ~adder) & (lead if leads else ~lead))
+                def _():
+                    drain(sums, (heads - is_adder_too) * (1 + leads), hr_sem.at[3])
+
+    for c in range(heads):
+        for t, out in enumerate((dk_ref, dv_ref)):
+            both = jnp.concatenate([sums[c, t], sums[heads + c, t]], axis=0)
+            extra = nn(hot_twice, both)
+            for i in range(nb):
+                rsl = slice(i * BLOCK, (i + 1) * BLOCK)
+                out[0, rsl, c * DH : (c + 1) * DH] = (own[c, i, t] + extra[rsl]).astype(BF16)
 
 
 def write_out(*refs):
@@ -541,7 +556,7 @@
                 pltpu.VMEM((2, gtok, DH), BF16),
                 pltpu.VMEM((2, gtok, DH), BF16),
                 pltpu.VMEM((2, gtok, DH), BF16),
-                pltpu.VMEM((heads, 2, gtok, DH), BF16),
+                pltpu.VMEM((2 * heads, 2, gtok, DH), BF16),
                 pltpu.SemaphoreType.DMA((2,)),
                 pltpu.VMEM((heads, nb, listed * BLOCK, group * BLOCK), F32),
                 pltpu.VMEM((heads, nb, listed * BLOCK, group * BLOCK), F32),

time: 25.9 us -> 24.8 us (0.958)
  Pallas kernels: 25 us -> 23.7 us
    pallas_call x1, Pallas kernels: 24.1 us -> 22.8 us  [local(): pl.pallas_call(functools.partial(kernel, n, heads, group, nb, listed, gto...]
where the time goes in v3:
time: 24.8 us; the launch traced here: 24.3 us
  Pallas kernels  23.7 us (96%)
  between operations  0.64 us (3%)
    pallas_call x1, Pallas kernels, local(): pl.pallas_call(functools.partial(kernel, n, heads, group, nb, listed, gto...  22.8 us
    pallas_call x1, Pallas kernels, local(): pl.pallas_call(write_out, out_shape=tuple((jax.ShapeDtypeStruct(a.shape,...  0.9 us

profile of v3, /device:TPU:0, one launch (start us, length us, event | category | flops | bytes accessed | tf_op | source)
XLA Modules:
  0.0 24.3 jit_solution(699243016498583292)
XLA Ops:
  0.6 22.8 %shard_map.94 = (bf16[1,256,1024]{2,1,0:T(8,128)(2,1)S(1)}, bf16[1,256,256]{2,1,0:T(8,128)(2,1)S(1)}, bf16[1,256,256]{2,1,0:T(8,128)(2,1)S(1)}) custom-call(s32[16]{0:T(128)} %owner_hbm.1, s32[1,2,3]{2,1,0:T(2,128)} %lists_hbm.1, s32[1,64]{1,0:T(1,128)} %goff_hbm.1, bf16[1,256,1024]{2,1,0:T(8,128)(2,1)} %q_hbm.1, bf16[1,256,256]{2,1,0:T(8,128)(2,1)} %k_hbm.1, ...), custom_call_target="tpu_custom_call" | custom-call | tf_op jit(solution)/shard_map/pallas_call | solution.py:536
  23.4 0.9 %shard_map.95 = (bf16[1,256,1024]{2,1,0:T(8,128)(2,1)}, bf16[1,256,256]{2,1,0:T(8,128)(2,1)}, bf16[1,256,256]{2,1,0:T(8,128)(2,1)}) custom-call(bf16[1,256,1024]{2,1,0:T(8,128)(2,1)S(1)} %get-tuple-element.6.refs_0_, bf16[1,256,256]{2,1,0:T(8,128)(2,1)S(1)} %get-tuple-element.7.refs_1_, bf16[1,256,256]{2,1,0:T(8,128)(2,1)S(1)} %get-tuple-element.8.refs_2_), custom_call_target="tpu_custom_call" | custom-call | tf_op jit(solution)/shard_map/pallas_call | solution.py:580

commit v4 on v3

--- a/solution.py
+++ b/solution.py
@@ -29,9 +29,9 @@
 def kernel(
     n, heads, group, nb, listed, gtok,
     owner_hbm, lists_hbm, goff_hbm, q_hbm, k_hbm, v_hbm, g_hbm,
-    dq_ref, dk_ref, dv_ref,
-    owner_ref, lists_ref, goff_ref, small_sem, qv, gv, gsend, hub_in, hub_out, gcand, gall, fw_sem, gpart, hub2_in, half_out, total_out, cross_in, sums, cross_sem,
-    keep_ex, keep_dp, keep_ds, wslot, own, sback, rback, load_sem, big_sem, ks_sem, kr_sem, gs_sem, gr_sem, hs_sem, hr_sem,
+    dq_ref, own, sums_out, hot_out,
+    owner_ref, lists_ref, goff_ref, small_sem, qv, gv, gsend, hub_in, hub_out, gcand, gall, fw_sem, gpart, hub2_in, half_out, total_out, cross_in, sums, sum_sem, cross_sem,
+    keep_ex, keep_dp, keep_ds, wslot, sback, rback, load_sem, big_sem, ks_sem, kr_sem, gs_sem, gr_sem, hs_sem, hr_sem,
     *kvw,
 ):
     me = lax.axis_index("seq")
@@ -51,16 +51,13 @@
     def hub_id(g, side):
         return first + 4 * row_of(g, side) + 2 * side
 
-    def sum_id(g, side):
-        return 4 * (g + side) + 2 * side + 1
-
-    def is_adder(i):
-        g = i // 4 - lax.rem(i // 2, 2)
-        return (g >= 0) & (g < heads) & (lax.rem(i, 2) == 1)
-
-    adder = is_adder(me)
-    sum_group = jnp.clip(me // 4 - col, 0, heads - 1)
-    other_sum = sum_id(sum_group, 1 - col)
+    def sum_id(t, side):
+        return 4 * jnp.where(side == 0, 1 + t, 2 - t) + 2 * side + 1
+
+    row = me // 4
+    adder = odd & (row > 0) & (row < 3)
+    sum_t = jnp.clip(jnp.where(col == 0, row - 1, 2 - row), 0, 1)
+    other_sum = sum_id(sum_t, 1 - col)
 
     def hubbed(i):
         return (i >= first) & (i < first + 2 * hubs) & (lax.rem(i + first, 2) == 0)
@@ -150,11 +147,10 @@
         rback[1] = jnp.zeros(rback.shape[1:], BF16)
 
     lead = me < LEADS
-    no_sum = jnp.zeros((2, gtok, DH), BF16)
-    for g in range(heads):
-        @pl.when(~lead | (adder & (sum_group == g)))
-        def _():
-            sums[heads + g] = no_sum
+
+    @pl.when(~lead)
+    def _():
+        sums[2 * heads :] = jnp.zeros((2 * heads, gtok, DH), BF16)
 
     zero_tile = jnp.zeros((nb, 2, BLOCK, DH), F32)
     wslot[:, listed] = zero_tile
@@ -303,9 +299,15 @@
             for c in range(1, heads):
                 halo_start(c, 0, False)
 
+    held_back = adder & (place == 3) & (other_sum > me)
+
     def back_start(c):
         for d in range(2):
-            each(d, False, lambda d=d: back(d, c).start())
+            if c == heads - 1 and d == 0:
+                ready = (me < n - 1) & ~held_back
+                pl.when(ready)(lambda d=d: back(d, c).start())
+            else:
+                each(d, False, lambda d=d: back(d, c).start())
 
     def drain_own(ref, count, sem, self_served):
         @pl.when(self_served)
@@ -375,9 +377,16 @@
             for t, part in enumerate((nn(ds, qs) * scale, nn(pr.astype(BF16), gs))):
                 glob[t] = part if glob[t] is None else glob[t] + part
         for t in range(2):
-            gpart[c, t] = glob[t].astype(BF16)
+            gpart[2 * c + t] = glob[t].astype(BF16)
         with jax.named_scope(f"s_gpart{c}"):
-            to_hub(gpart, hub2_in, 2, c, sum_id(c, col))
+            for t in range(2):
+                target = sum_id(t, col)
+
+                @pl.when(me != target)
+                def _():
+                    remote(
+                        gpart.at[2 * c + t], hub2_in.at[c, lane], hs_sem.at[2], sum_sem.at[c], target
+                    ).start()
 
     for c in range(heads):
         for b in range(nb):
@@ -423,35 +432,43 @@
     def give(src, target, at):
         remote(src, sums.at[at], hs_sem.at[3], hr_sem.at[3], target).start()
 
+    def cross(c):
+        return remote(
+            half_out.at[c], cross_in.at[c], cross_sem.at[c], cross_sem.at[heads + c], other_sum
+        )
+
     @pl.when(adder)
     def _():
-        with jax.named_scope("w_hub2"):
-            drain(hub2_in, n // 2 - 1, hr_sem.at[2])
-        hub2_in[lane] = gpart[sum_group]
-        half = jnp.sum(hub2_in[...].astype(F32), axis=0)
-        half_out[...] = half.astype(BF16)
-        cross = remote(half_out, cross_in, cross_sem.at[0], cross_sem.at[1], other_sum)
-        cross.start()
-        for target in range(LEADS):
-            @pl.when((me != target) & (other_sum != target))
-            def _():
-                give(half_out, target, col * heads + sum_group)
-
-        with jax.named_scope("w_cross"):
-            cross.wait_recv()
-        total = (half + cross_in[...].astype(F32)).astype(BF16)
-        total_out[...] = total
-        sums[sum_group] = total
-
-        @pl.loop(0, n // 2)
-        def _(k):
-            target = 4 * far_first(k // 2, n // 4) + col * 2 + lax.rem(k, 2)
-
-            @pl.when((target != me) & (target >= LEADS))
-            def _():
-                give(total_out, target, sum_group)
-
-        cross.wait_send()
+        halves = []
+        for c in range(heads):
+            with jax.named_scope(f"w_hub2{c}"):
+                drain(hub2_in.at[c], n // 2 - 1, sum_sem.at[c])
+            hub2_in[c, lane] = gpart[2 * c + sum_t]
+            half = jnp.sum(hub2_in[c].astype(F32), axis=0)
+            halves.append(half)
+            half_out[c] = half.astype(BF16)
+            cross(c).start()
+            for target in range(LEADS):
+                give(half_out.at[c], target, 2 * (col * heads + c) + sum_t)
+
+        @pl.when(held_back)
+        def _():
+            back(0, heads - 1).start()
+
+        for c in range(heads):
+            with jax.named_scope(f"w_cross{c}"):
+                cross(c).wait_recv()
+            total = (halves[c] + cross_in[c].astype(F32)).astype(BF16)
+            total_out[c] = total
+            sums[2 * c + sum_t] = total
+
+            @pl.loop(0, n // 2)
+            def _(k):
+                target = 4 * far_first(k // 2, n // 4) + col * 2 + lax.rem(k, 2)
+
+                @pl.when((target != me) & (target >= LEADS))
+                def _():
+                    give(total_out.at[c], target, 2 * c + sum_t)
 
     for c in range(heads):
         with jax.named_scope(f"w_back{c}"):
@@ -463,7 +480,7 @@
                 own[c, i, t] = own[c, i, t] + total
 
     flag = jnp.where(owner_ref[0] == me, 1.0, 0.0)
-    hot_twice = (jnp.concatenate([hot, hot], axis=1).astype(F32) * flag).astype(BF16)
+    hot_out[...] = (jnp.concatenate([hot, hot], axis=1).astype(F32) * flag).astype(BF16)
 
     for c in range(heads):
         for d in range(2):
@@ -481,38 +498,44 @@
 
     @pl.when(adder)
     def _():
-        drain(hub2_in, n // 2 - 1, hs_sem.at[3])
-
-    for extra_sends in (1, LEADS):
-        @pl.when(adder & (col == 1) & ((other_sum < LEADS) == (extra_sends < LEADS)))
+        for c in range(heads):
+            drain(hub2_in.at[c], n // 2 - 1, hs_sem.at[3])
+            cross(c).wait_send()
+
+    @pl.when(adder & (col == 1))
+    def _():
+        drain(gpart, LEADS * heads, hs_sem.at[3])
+
+    drain_own(gsend, heads, hs_sem.at[0], mine_hub)
+    for self_served in range(2):
+        @pl.when(adder if self_served else ~adder)
         def _():
-            drain(hub2_in, extra_sends, hs_sem.at[3])
-
-    drain_own(gsend, heads, hs_sem.at[0], mine_hub)
-    drain_own(gpart, heads, hs_sem.at[2], adder)
+            drain(gpart, heads * (2 - self_served), hs_sem.at[2])
+
 
     with jax.named_scope("w_gall2"):
-        for is_adder_too in range(2):
-            for leads in range(2):
-                @pl.when((adder if is_adder_too else ~adder) & (lead if leads else ~lead))
-                def _():
-                    drain(sums, (heads - is_adder_too) * (1 + leads), hr_sem.at[3])
-
-    for c in range(heads):
-        for t, out in enumerate((dk_ref, dv_ref)):
-            both = jnp.concatenate([sums[c, t], sums[heads + c, t]], axis=0)
-            extra = nn(hot_twice, both)
-            for i in range(nb):
+        for who, count in ((lead, 4), (adder, 1), (~lead & ~adder, 2)):
+            @pl.when(who)
+            def _():
+                drain(sums, count * heads, hr_sem.at[3])
+
+    sums_out[...] = sums[...]
+
+
+def write_out(heads, dq_ref, own, sums, hot, dq_out, dk_out, dv_out, dk_ref, dv_ref, sem):
+    first = pltpu.make_async_copy(dq_ref, dq_out, sem.at[0])
+    first.start()
+    copies = [first]
+    for t, (held, out) in enumerate(((dk_ref, dk_out), (dv_ref, dv_out))):
+        for c in range(heads):
+            both = jnp.concatenate([sums[2 * c + t], sums[2 * (heads + c) + t]], axis=0)
+            extra = nn(hot[...], both)
+            for i in range(own.shape[1]):
                 rsl = slice(i * BLOCK, (i + 1) * BLOCK)
-                out[0, rsl, c * DH : (c + 1) * DH] = (own[c, i, t] + extra[rsl]).astype(BF16)
-
-
-def write_out(*refs):
-    copies = [
-        pltpu.make_async_copy(refs[i], refs[3 + i], refs[6].at[i]) for i in range(3)
-    ]
-    for cp in copies:
+                held[0, rsl, c * DH : (c + 1) * DH] = (own[c, i, t] + extra[rsl]).astype(BF16)
+        cp = pltpu.make_async_copy(held, out, sem.at[1 + t])
         cp.start()
+        copies.append(cp)
     for cp in copies:
         cp.wait()
 
@@ -535,9 +558,14 @@
         hb = pl.BlockSpec(memory_space=pl.ANY)
         held = pl.pallas_call(
             functools.partial(kernel, n, heads, group, nb, listed, gtok),
-            out_shape=tuple(pltpu.VMEM(a.shape, BF16) for a in (query, keys, values)),
+            out_shape=(
+                pltpu.VMEM(query.shape, BF16),
+                pltpu.VMEM((heads, nb, 2, BLOCK, DH), F32),
+                pltpu.VMEM((4 * heads, gtok, DH), BF16),
+                pltpu.VMEM((rows, 2 * gtok), BF16),
+            ),
             in_specs=[hb] * 7,
-            out_specs=(vm, vm, vm),
+            out_specs=(vm,) * 4,
             scratch_shapes=[
                 pltpu.SMEM(owner.shape, jnp.int32),
                 pltpu.SMEM(block_lists.shape, jnp.int32),
@@ -551,18 +579,18 @@
                 pltpu.VMEM((2 * heads, 2, gtok, DH), BF16),
                 pltpu.VMEM((heads, 2, gtok, DH), BF16),
                 pltpu.SemaphoreType.DMA((2,)),
-                pltpu.VMEM((heads, 2, gtok, DH), BF16),
-                pltpu.VMEM((n // 2, 2, gtok, DH), BF16),
-                pltpu.VMEM((2, gtok, DH), BF16),
-                pltpu.VMEM((2, gtok, DH), BF16),
-                pltpu.VMEM((2, gtok, DH), BF16),
-                pltpu.VMEM((2 * heads, 2, gtok, DH), BF16),
-                pltpu.SemaphoreType.DMA((2,)),
+                pltpu.VMEM((2 * heads, gtok, DH), BF16),
+                pltpu.VMEM((heads, n // 2, gtok, DH), BF16),
+                pltpu.VMEM((heads, gtok, DH), BF16),
+                pltpu.VMEM((heads, gtok, DH), BF16),
+                pltpu.VMEM((heads, gtok, DH), BF16),
+                pltpu.VMEM((4 * heads, gtok, DH), BF16),
+                pltpu.SemaphoreType.DMA((heads,)),
+                pltpu.SemaphoreType.DMA((2 * heads,)),
                 pltpu.VMEM((heads, nb, listed * BLOCK, group * BLOCK), F32),
                 pltpu.VMEM((heads, nb, listed * BLOCK, group * BLOCK), F32),
                 pltpu.VMEM((heads, nb, listed * BLOCK + gtok, group * BLOCK), BF16),
                 pltpu.VMEM((nb, listed + 1, 2, BLOCK, DH), F32),
-                pltpu.VMEM((heads, nb, 2, BLOCK, DH), F32),
                 pltpu.VMEM((2, heads, REACH, 2, BLOCK, DH), BF16),
                 pltpu.VMEM((2, heads, REACH, 2, BLOCK, DH), BF16),
                 pltpu.SemaphoreType.DMA((2 * heads * nb,)),
@@ -578,11 +606,15 @@
             compiler_params=pltpu.CompilerParams(collective_id=0, has_side_effects=True),
         )(owner, block_lists, global_offset, query, keys, values, grad_out)
         return pl.pallas_call(
-            write_out,
+            functools.partial(write_out, heads),
             out_shape=tuple(jax.ShapeDtypeStruct(a.shape, BF16) for a in (query, keys, values)),
-            in_specs=[hb] * 3,
+            in_specs=[hb, vm, vm, vm],
             out_specs=[hb] * 3,
-            scratch_shapes=[pltpu.SemaphoreType.DMA((3,))],
+            scratch_shapes=[
+                pltpu.VMEM(keys.shape, BF16),
+                pltpu.VMEM(values.shape, BF16),
+                pltpu.SemaphoreType.DMA((3,)),
+            ],
         )(*[pltpu.with_memory_space_constraint(a, pltpu.VMEM) for a in held])
 
     return jax.shard_map(

time: 24.8 us -> 24 us (0.968)
  the two profiles are of different devices: /device:TPU:0 before, /device:TPU:3 now
where the time goes in v4:
time: 24 us; the launch traced here: 23.8 us
  Pallas kernels  23.1 us (96%)
  between operations  0.64 us (3%)
    pallas_call x1, Pallas kernels, local(): pl.pallas_call(functools.partial(kernel, n, heads, group, nb, listed, gto...  22.2 us
    pallas_call x1, Pallas kernels, local(): pl.pallas_call(functools.partial(write_out, heads), out_shape=tuple((jax....  0.91 us

profile of v4, /device:TPU:3, one launch (start us, length us, event | category | flops | bytes accessed | tf_op | source)
XLA Modules:
  0.0 23.8 jit_solution(6040667321534884829)
XLA Ops:
  0.6 22.2 %shard_map.94 = (bf16[1,256,1024]{2,1,0:T(8,128)(2,1)S(1)}, f32[2,2,2,128,128]{4,3,2,1,0:T(8,128)S(1)}, bf16[8,64,128]{2,1,0:T(8,128)(2,1)S(1)}, bf16[256,128]{1,0:T(8,128)(2,1)S(1)}) custom-call(s32[16]{0:T(128)} %owner_hbm.1, s32[1,2,3]{2,1,0:T(2,128)} %lists_hbm.1, s32[1,64]{1,0:T(1,128)} %goff_hbm.1, bf16[1,256,1024]{2,1,0:T(8,128)(2,1)} %q_hbm.1, ...), custom_call_target="tpu_custom_call" | custom-call | tf_op jit(solution)/shard_map/pallas_call | solution.py:559
  22.9 0.9 %shard_map.95 = (bf16[1,256,1024]{2,1,0:T(8,128)(2,1)}, bf16[1,256,256]{2,1,0:T(8,128)(2,1)}, bf16[1,256,256]{2,1,0:T(8,128)(2,1)}) custom-call(bf16[1,256,1024]{2,1,0:T(8,128)(2,1)S(1)} %get-tuple-element.7.dq_ref, f32[2,2,2,128,128]{4,3,2,1,0:T(8,128)S(1)} %get-tuple-element.8.own, bf16[8,64,128]{2,1,0:T(8,128)(2,1)S(1)} %get-tuple-element.9.sums, ...), custom_call_target="tpu_custom_call" | custom-call | tf_op jit(solution)/shard_map/pallas_call | solution.py:608

commit v5 on v4

--- a/solution.py
+++ b/solution.py
@@ -30,10 +30,11 @@
     n, heads, group, nb, listed, gtok,
     owner_hbm, lists_hbm, goff_hbm, q_hbm, k_hbm, v_hbm, g_hbm,
     dq_ref, own, sums_out, hot_out,
-    owner_ref, lists_ref, goff_ref, small_sem, qv, gv, gsend, hub_in, hub_out, gcand, gall, fw_sem, gpart, hub2_in, half_out, total_out, cross_in, sums, sum_sem, cross_sem,
+    owner_ref, lists_ref, goff_ref, small_sem, qv, gv, gsend, hub_in, hub_out, cand_sem, gall, fw_sem, gpart, hub2_in, half_out, total_out, cross_in, sums, sum_sem, cross_sem,
     keep_ex, keep_dp, keep_ds, wslot, sback, rback, load_sem, big_sem, ks_sem, kr_sem, gs_sem, gr_sem, hs_sem, hr_sem,
-    *kvw,
+    *rest,
 ):
+    kvw, gcand = rest[: 2 * heads], rest[2 * heads :]
     me = lax.axis_index("seq")
     hubs = 2 * heads
     rows = nb * BLOCK
@@ -131,7 +132,7 @@
         for c in range(heads):
             mine = kvw[t * heads + c][REACH : REACH + nb].reshape(rows, DH)
             got = lax.dot_general(hot, mine, (((0,), (0,)), ((), ())), preferred_element_type=F32)
-            gsend[c, t] = got.astype(BF16)
+            gsend[t, c] = got.astype(BF16)
     zeros_kv = jnp.zeros((REACH, BLOCK, DH), BF16)
 
     @pl.when(me == 0)
@@ -282,17 +283,19 @@
         hub_in[lane] = gsend[group_of]
         pick = hub_in[(owner_at // 4) * 2 + lax.rem(owner_at, 2)]
         hub_out[...] = pick
-        gcand[col * heads + group_of] = pick
-
-        @pl.loop(0, n // 2)
-        def _(k):
-            target = 4 * far_first(k // 2, n // 4) + 2 * lax.rem(k, 2) + 1
-
-            @pl.when(target != me)
-            def _():
-                remote(
-                    hub_out, gcand.at[col * heads + group_of], hs_sem.at[1], hr_sem.at[1], target
-                ).start()
+        for c in range(heads):
+            gcand[c][2 * col + group_of] = pick[c]
+        for c in range(heads):
+            @pl.loop(0, n // 2)
+            def _(k):
+                target = 4 * far_first(k // 2, n // 4) + 2 * lax.rem(k, 2) + 1
+
+                @pl.when(target != me)
+                def _():
+                    remote(
+                        hub_out.at[c], gcand[c].at[2 * col + group_of],
+                        hs_sem.at[1], cand_sem.at[c], target,
+                    ).start()
 
         @pl.when(held)
         def _():
@@ -318,17 +321,56 @@
         def _():
             drain(ref, count, sem)
 
-    pass_on = remote(gall, gall, fw_sem.at[0], fw_sem.at[1], jnp.where(odd, me - 1, me + 1))
+    def pass_on(c):
+        return remote(
+            gall.at[c], gall.at[c], fw_sem.at[c], fw_sem.at[heads + c],
+            jnp.where(odd, me - 1, me + 1),
+        )
 
     def collect():
-        with jax.named_scope("w_cand"):
-            drain_own(gcand, 2 * heads, hr_sem.at[1], mine_hub)
-        side = lax.rem(owner_at // 2, 2) * heads
-        for g in range(heads):
-            gall[g] = gcand[side + g]
-        pass_on.start()
+        side = lax.rem(owner_at // 2, 2) * 2
+        for c in range(heads):
+            with jax.named_scope(f"w_cand{c}"):
+                drain_own(gcand[c], 4, cand_sem.at[c], mine_hub)
+            for t in range(2):
+                gall[c, t] = gcand[c][side + t]
+            pass_on(c).start()
 
     ratios = {}
+
+    def key_value_grads(c):
+        for b in range(nb):
+            qs, gs = stacked(qv, c, b), stacked(gv, c, b)
+            own_ratio, near_ratio, dot = ratios[c, b]
+            vals = []
+            for lo, hi, ratio in ((0, BLOCK, own_ratio), (BLOCK, window, near_ratio)):
+                pr = keep_ex[c, b, lo:hi] * ratio
+                ds = (pr * (keep_dp[c, b, lo:hi] - dot)).astype(BF16)
+                keep_ds[c, b, lo:hi] = ds
+                vals.append((ds, pr.astype(BF16)))
+            ds, pr = (jnp.concatenate([v[i] for v in vals], axis=0) for i in range(2))
+            for t, val in enumerate((nn(ds, qs) * scale, nn(pr, gs))):
+                for l in range(listed):
+                    wslot[b, l, t] = val[l * BLOCK : (l + 1) * BLOCK]
+        for dst in range(nb + 2 * REACH):
+            total = None
+            for b in range(nb):
+                if not b <= dst <= b + 2 * REACH:
+                    continue
+                slot = jnp.int32(listed)
+                for l in range(1, listed):
+                    slot = jnp.where(local_idx[b][l] == dst, l, slot)
+                term = wslot[b, 0] if dst == b + REACH else wslot[b, slot]
+                total = term if total is None else total + term
+            if dst < REACH:
+                sback[1, c, dst] = total.astype(BF16)
+            elif dst < REACH + nb:
+                own[c, dst - REACH] = total
+            else:
+                sback[0, c, dst - REACH - nb] = total.astype(BF16)
+        with jax.named_scope(f"s_back{c}"):
+            back_start(c)
+
     for c in range(heads):
         last = c == heads - 1
         with jax.named_scope(f"w_halo{c}"):
@@ -341,10 +383,10 @@
                 stats[c, b].append(keep(c, b, BLOCK, *logits(kn, vn, c, b)))
         if c == 0:
             pl.when(odd)(collect)
-            with jax.named_scope("w_gall"):
-                @pl.when(~odd)
-                def _():
-                    pass_on.wait_recv()
+        with jax.named_scope(f"w_gall{c}"):
+            @pl.when(~odd)
+            def _():
+                pass_on(c).wait_recv()
         glob = [None, None]
         for b in range(nb):
             qs, gs = stacked(qv, c, b), stacked(gv, c, b)
@@ -387,39 +429,12 @@
                     remote(
                         gpart.at[2 * c + t], hub2_in.at[c, lane], hs_sem.at[2], sum_sem.at[c], target
                     ).start()
-
-    for c in range(heads):
-        for b in range(nb):
-            qs, gs = stacked(qv, c, b), stacked(gv, c, b)
-            own_ratio, near_ratio, dot = ratios[c, b]
-            vals = []
-            for lo, hi, ratio in ((0, BLOCK, own_ratio), (BLOCK, window, near_ratio)):
-                pr = keep_ex[c, b, lo:hi] * ratio
-                ds = (pr * (keep_dp[c, b, lo:hi] - dot)).astype(BF16)
-                keep_ds[c, b, lo:hi] = ds
-                vals.append((ds, pr.astype(BF16)))
-            ds, pr = (jnp.concatenate([v[i] for v in vals], axis=0) for i in range(2))
-            for t, val in enumerate((nn(ds, qs) * scale, nn(pr, gs))):
-                for l in range(listed):
-                    wslot[b, l, t] = val[l * BLOCK : (l + 1) * BLOCK]
-        for dst in range(nb + 2 * REACH):
-            total = None
-            for b in range(nb):
-                if not b <= dst <= b + 2 * REACH:
-                    continue
-                slot = jnp.int32(listed)
-                for l in range(1, listed):
-                    slot = jnp.where(local_idx[b][l] == dst, l, slot)
-                term = wslot[b, 0] if dst == b + REACH else wslot[b, slot]
-                total = term if total is None else total + term
-            if dst < REACH:
-                sback[1, c, dst] = total.astype(BF16)
-            elif dst < REACH + nb:
-                own[c, dst - REACH] = total
-            else:
-                sback[0, c, dst - REACH - nb] = total.astype(BF16)
-        with jax.named_scope(f"s_back{c}"):
-            back_start(c)
+        if c == 0:
+            pl.when(odd)(functools.partial(key_value_grads, 0))
+
+    pl.when(~odd)(functools.partial(key_value_grads, 0))
+    for c in range(1, heads):
+        key_value_grads(c)
 
     for c in range(heads):
         for b in range(nb):
@@ -490,7 +505,8 @@
 
     @pl.when(odd)
     def _():
-        pass_on.wait_send()
+        for c in range(heads):
+            pass_on(c).wait_send()
 
     @pl.when(mine_hub)
     def _():
@@ -553,7 +569,7 @@
         gtok = global_offset.shape[1]
         hubs = 2 * heads
         wide = nb + 2 * REACH
-        assert nb == REACH and n % 8 == 0 and n >= 2 * hubs and heads % 2 == 0
+        assert nb == REACH and n % 8 == 0 and n >= 4 * hubs and heads == 2
         vm = pl.BlockSpec(memory_space=pltpu.VMEM)
         hb = pl.BlockSpec(memory_space=pl.ANY)
         held = pl.pallas_call(
@@ -573,12 +589,12 @@
                 pltpu.SemaphoreType.DMA((3,)),
                 pltpu.VMEM((rows, qw), BF16),
                 pltpu.VMEM((rows, qw), BF16),
+                pltpu.VMEM((2, heads, gtok, DH), BF16),
+                pltpu.VMEM((n // 2, heads, gtok, DH), BF16),
+                pltpu.VMEM((heads, gtok, DH), BF16),
+                pltpu.SemaphoreType.DMA((heads,)),
                 pltpu.VMEM((heads, 2, gtok, DH), BF16),
-                pltpu.VMEM((n // 2, 2, gtok, DH), BF16),
-                pltpu.VMEM((2, gtok, DH), BF16),
-                pltpu.VMEM((2 * heads, 2, gtok, DH), BF16),
-                pltpu.VMEM((heads, 2, gtok, DH), BF16),
-                pltpu.SemaphoreType.DMA((2,)),
+                pltpu.SemaphoreType.DMA((2 * heads,)),
                 pltpu.VMEM((2 * heads, gtok, DH), BF16),
                 pltpu.VMEM((heads, n // 2, gtok, DH), BF16),
                 pltpu.VMEM((heads, gtok, DH), BF16),
@@ -602,7 +618,8 @@
                 pltpu.SemaphoreType.DMA((4,)),
                 pltpu.SemaphoreType.DMA((4,)),
             ]
-            + [pltpu.VMEM((wide, BLOCK, DH), BF16)] * (2 * heads),
+            + [pltpu.VMEM((wide, BLOCK, DH), BF16)] * (2 * heads)
+            + [pltpu.VMEM((4, gtok, DH), BF16)] * heads,
             compiler_params=pltpu.CompilerParams(collective_id=0, has_side_effects=True),
         )(owner, block_lists, global_offset, query, keys, values, grad_out)
         return pl.pallas_call(

time: 24 us -> 23.7 us (0.987)
  the two profiles are of different devices: /device:TPU:3 before, /device:TPU:0 now
where the time goes in v5:
time: 23.7 us; the launch traced here: 23.3 us
  Pallas kernels  22.7 us (96%)
  between operations  0.64 us (3%)
    pallas_call x1, Pallas kernels, local(): pl.pallas_call(functools.partial(kernel, n, heads, group, nb, listed, gto...  21.8 us
    pallas_call x1, Pallas kernels, local(): pl.pallas_call(functools.partial(write_out, heads), out_shape=tuple((jax....  0.91 us

profile of v5, /device:TPU:0, one launch (start us, length us, event | category | flops | bytes accessed | tf_op | source)
XLA Modules:
  0.0 23.3 jit_solution(1148140559868600792)
XLA Ops:
  0.6 21.8 %shard_map.94 = (bf16[1,256,1024]{2,1,0:T(8,128)(2,1)S(1)}, f32[2,2,2,128,128]{4,3,2,1,0:T(8,128)S(1)}, bf16[8,64,128]{2,1,0:T(8,128)(2,1)S(1)}, bf16[256,128]{1,0:T(8,128)(2,1)S(1)}) custom-call(s32[16]{0:T(128)} %owner_hbm.1, s32[1,2,3]{2,1,0:T(2,128)} %lists_hbm.1, s32[1,64]{1,0:T(1,128)} %goff_hbm.1, bf16[1,256,1024]{2,1,0:T(8,128)(2,1)} %q_hbm.1, ...), custom_call_target="tpu_custom_call" | custom-call | tf_op jit(solution)/shard_map/pallas_call | solution.py:575
  22.4 0.9 %shard_map.95 = (bf16[1,256,1024]{2,1,0:T(8,128)(2,1)}, bf16[1,256,256]{2,1,0:T(8,128)(2,1)}, bf16[1,256,256]{2,1,0:T(8,128)(2,1)}) custom-call(bf16[1,256,1024]{2,1,0:T(8,128)(2,1)S(1)} %get-tuple-element.7.dq_ref, f32[2,2,2,128,128]{4,3,2,1,0:T(8,128)S(1)} %get-tuple-element.8.own, bf16[8,64,128]{2,1,0:T(8,128)(2,1)S(1)} %get-tuple-element.9.sums, ...), custom_call_target="tpu_custom_call" | custom-call | tf_op jit(solution)/shard_map/pallas_call | solution.py:625

commit v6 on v5

--- a/solution.py
+++ b/solution.py
@@ -479,7 +479,7 @@
 
             @pl.loop(0, n // 2)
             def _(k):
-                target = 4 * far_first(k // 2, n // 4) + col * 2 + lax.rem(k, 2)
+                target = 4 * (k // 2) + col * 2 + lax.rem(k, 2)
 
                 @pl.when((target != me) & (target >= LEADS))
                 def _():

time: 23.7 us -> 23.7 us (level)
  no operation moved by 1% of the time
where the time goes in v6:
time: 23.7 us; the launch traced here: 23.3 us
  Pallas kernels  22.7 us (96%)
  between operations  0.64 us (3%)
    pallas_call x1, Pallas kernels, local(): pl.pallas_call(functools.partial(kernel, n, heads, group, nb, listed, gto...  21.8 us
    pallas_call x1, Pallas kernels, local(): pl.pallas_call(functools.partial(write_out, heads), out_shape=tuple((jax....  0.91 us

profile of v6, /device:TPU:0, one launch (start us, length us, event | category | flops | bytes accessed | tf_op | source)
XLA Modules:
  0.0 23.3 jit_solution(18174906229094155518)
XLA Ops:
  0.6 21.8 %shard_map.94 = (bf16[1,256,1024]{2,1,0:T(8,128)(2,1)S(1)}, f32[2,2,2,128,128]{4,3,2,1,0:T(8,128)S(1)}, bf16[8,64,128]{2,1,0:T(8,128)(2,1)S(1)}, bf16[256,128]{1,0:T(8,128)(2,1)S(1)}) custom-call(s32[16]{0:T(128)} %owner_hbm.1, s32[1,2,3]{2,1,0:T(2,128)} %lists_hbm.1, s32[1,64]{1,0:T(1,128)} %goff_hbm.1, bf16[1,256,1024]{2,1,0:T(8,128)(2,1)} %q_hbm.1, ...), custom_call_target="tpu_custom_call" | custom-call | tf_op jit(solution)/shard_map/pallas_call | solution.py:575
  22.4 0.9 %shard_map.95 = (bf16[1,256,1024]{2,1,0:T(8,128)(2,1)}, bf16[1,256,256]{2,1,0:T(8,128)(2,1)}, bf16[1,256,256]{2,1,0:T(8,128)(2,1)}) custom-call(bf16[1,256,1024]{2,1,0:T(8,128)(2,1)S(1)} %get-tuple-element.7.dq_ref, f32[2,2,2,128,128]{4,3,2,1,0:T(8,128)S(1)} %get-tuple-element.8.own, bf16[8,64,128]{2,1,0:T(8,128)(2,1)S(1)} %get-tuple-element.9.sums, ...), custom_call_target="tpu_custom_call" | custom-call | tf_op jit(solution)/shard_map/pallas_call | solution.py:625
